TPU v7x, 32 devices: a 4x2x2 block of a 4x4x8 slice. The times are simulated.
32 devices in a mesh: dp: 4 (over y, z), sp: 8 (over x, core).
Axes of the slice: x: 4, y: 2, z: 2, core: 2. Of those that a mesh axis runs over, the one named last changes fastest.
The devices are a block of a 4x4x8 slice.
Arguments:
- x_tok: bfloat16 [32768, 1536], P(('dp', 'sp')), parts along dimension 0
- doc_start: int32 [32768], P(('dp', 'sp')), parts along dimension 0
- w_q: bfloat16 [1536, 24, 64], replicated
- w_k: bfloat16 [1536, 24, 64], replicated
- w_v: bfloat16 [1536, 24, 64], replicated
- w_o: bfloat16 [24, 64, 1536], replicated
- dy_tok: bfloat16 [32768, 1536], P(('dp', 'sp')), parts along dimension 0
Outputs:
- output 1: bfloat16 [32768, 1536], P(('dp', 'sp')), parts along dimension 0
- output 2: bfloat16 [32768, 1536], P(('dp', 'sp')), parts along dimension 0
- output 3: float32 [6144, 24, 64], P('dp'), parts along dimension 0
- output 4: float32 [6144, 24, 64], P('dp'), parts along dimension 0
- output 5: float32 [6144, 24, 64], P('dp'), parts along dimension 0
- output 6: float32 [96, 64, 1536], P('dp'), parts along dimension 0
There are 4 independent parts. A program takes and returns all parts, laid end to end along the dimension named above; an argument that names none is the same for every part.
All inputs are finite; a program needn't handle non-finite values.
Results may differ from a plain program's by a relative error of at most 0.00188113.
Values are sent between devices in bfloat16 or wider.
A program may use at most 768 MiB of HBM per device.

v0:
```python
import math
import jax
import jax.numpy as jnp
from jax import lax
from jax.sharding import PartitionSpec as P


def block_masks(flag_loc):
    tok_count = flag_loc.shape[0]
    positions = jnp.arange(tok_count)
    seg_ids = jnp.cumsum(flag_loc)
    first_pos = jnp.min(jnp.where(flag_loc > 0, positions, tok_count))
    last_pos = jnp.max(jnp.where(flag_loc > 0, positions, -1))
    head_col = (positions < first_pos)[:, None, None]
    tail_col = (positions >= last_pos)[:, None, None]
    same_doc = (seg_ids[:, None] == seg_ids[None, :]) & (positions[None, :] <= positions[:, None])
    doc_gate = (last_pos < 0).astype(jnp.float32)
    return head_col, tail_col, same_doc, doc_gate


def solution(mesh):
    seq_devs = mesh.shape['sp']
    fwd_perm = [(src_rank, src_rank + 1) for src_rank in range(seq_devs - 1)]
    bwd_perm = [(src_rank + 1, src_rank) for src_rank in range(seq_devs - 1)]

    def pass_state(local_state, doc_gate, perm_list):
        def hop_step(step_idx, hop_carry):
            return lax.ppermute(doc_gate * hop_carry + local_state, 'sp', perm_list)
        return lax.fori_loop(0, seq_devs - 1, hop_step, jnp.zeros_like(local_state))

    def device_body(x_loc, flag_loc, w_q, w_k, w_v, w_o, dy_loc):
        tok_count = x_loc.shape[0]
        head_dim = w_q.shape[2]
        score_scale = 1.0 / (math.sqrt(head_dim) * tok_count)
        head_col, tail_col, same_doc, doc_gate = block_masks(flag_loc)
        q_rows = jnp.einsum('td,dhk->thk', x_loc, w_q, preferred_element_type=jnp.float32).astype(jnp.bfloat16)
        k_rows = jnp.einsum('td,dhk->thk', x_loc, w_k, preferred_element_type=jnp.float32).astype(jnp.bfloat16)
        v_rows = jnp.einsum('td,dhk->thk', x_loc, w_v, preferred_element_type=jnp.float32).astype(jnp.bfloat16)
        scores = jnp.einsum('thk,shk->hts', q_rows, k_rows, preferred_element_type=jnp.float32)
        attn_prob = jnp.where(same_doc, scores * score_scale, 0.0).astype(jnp.bfloat16)
        m_tail = jnp.einsum('til,tiw->ilw', k_rows, jnp.where(tail_col, v_rows, 0.0), preferred_element_type=jnp.float32)
        fwd_state = pass_state(m_tail, doc_gate, fwd_perm)
        state_low = fwd_state.astype(jnp.bfloat16)
        intra_sum = jnp.einsum('hts,shv->thv', attn_prob, v_rows, preferred_element_type=jnp.float32)
        inter_sum = jnp.einsum('uil,ilw->uiw', q_rows, state_low, preferred_element_type=jnp.float32)
        out_rows = (intra_sum + jnp.where(head_col, inter_sum * score_scale, 0.0)).astype(jnp.bfloat16)
        y_loc = jnp.einsum('thk,hkc->tc', out_rows, w_o, preferred_element_type=jnp.float32).astype(jnp.bfloat16)
        d_out = jnp.einsum('tc,hkc->thk', dy_loc, w_o, preferred_element_type=jnp.float32).astype(jnp.bfloat16)
        n_head = jnp.einsum('uil,uiw->ilw', q_rows, jnp.where(head_col, d_out, 0.0), preferred_element_type=jnp.float32)
        rev_state = pass_state(n_head, doc_gate, bwd_perm)
        rev_low = rev_state.astype(jnp.bfloat16)
        dp_raw = jnp.einsum('thv,shv->hts', d_out, v_rows, preferred_element_type=jnp.float32)
        d_prob = jnp.where(same_doc, dp_raw * score_scale, 0.0).astype(jnp.bfloat16)
        dq_rows = (jnp.einsum('hts,shk->thk', d_prob, k_rows, preferred_element_type=jnp.float32)
                   + jnp.where(head_col, jnp.einsum('uiw,ilw->uil', d_out, state_low, preferred_element_type=jnp.float32) * score_scale, 0.0)).astype(jnp.bfloat16)
        dk_rows = (jnp.einsum('hts,thk->shk', d_prob, q_rows, preferred_element_type=jnp.float32)
                   + jnp.where(tail_col, jnp.einsum('tiw,ilw->til', v_rows, rev_low, preferred_element_type=jnp.float32) * score_scale, 0.0)).astype(jnp.bfloat16)
        dv_rows = (jnp.einsum('hts,thv->shv', attn_prob, d_out, preferred_element_type=jnp.float32)
                   + jnp.where(tail_col, jnp.einsum('til,ilw->tiw', k_rows, rev_low, preferred_element_type=jnp.float32) * score_scale, 0.0)).astype(jnp.bfloat16)
        dx_loc = (jnp.einsum('thk,dhk->td', dq_rows, w_q, preferred_element_type=jnp.float32)
                  + jnp.einsum('thk,dhk->td', dk_rows, w_k, preferred_element_type=jnp.float32)
                  + jnp.einsum('thk,dhk->td', dv_rows, w_v, preferred_element_type=jnp.float32)).astype(jnp.bfloat16)
        dw_q = jnp.einsum('td,thk->dhk', x_loc, dq_rows, preferred_element_type=jnp.float32)
        dw_k = jnp.einsum('td,thk->dhk', x_loc, dk_rows, preferred_element_type=jnp.float32)
        dw_v = jnp.einsum('td,thk->dhk', x_loc, dv_rows, preferred_element_type=jnp.float32)
        dw_o = jnp.einsum('thk,tc->hkc', out_rows, dy_loc, preferred_element_type=jnp.float32)
        dw_q, dw_k, dw_v, dw_o = lax.psum((dw_q, dw_k, dw_v, dw_o), 'sp')
        return y_loc, dx_loc, dw_q, dw_k, dw_v, dw_o

    row_spec = P(('dp', 'sp'), None)
    flag_spec = P(('dp', 'sp'))
    w_spec = P(None, None, None)
    dw_spec = P('dp', None, None)
    mapped = jax.shard_map(device_body, mesh=mesh,
                           in_specs=(row_spec, flag_spec, w_spec, w_spec, w_spec, w_spec, row_spec),
                           out_specs=(row_spec, row_spec, dw_spec, dw_spec, dw_spec, dw_spec),
                           check_vma=False)
    return mapped
```

profile of v0, /device:TPU:81, one launch (start us, length us, event | category | flops | bytes accessed | tf_op | source)
XLA Modules:
  0.0 872.9 jit_solution(1628596336319661683)
XLA Ops:
  11.6 7.0 fusion.30
  20.8 5.1 fusion.32
  28.1 5.1 fusion.31
  36.1 6.6 fusion.19
  42.8 22.7 %select_convert_fusion.1 = bf16[24,1024,1024]{2,1,0:T(8,128)(2,1)} fusion(pred[1024,1024]{1,0:T(8,128)(4,1)} %fusion.1, bf16[1024,24,64]{0,2,1:T(8,128)(2,1)} %convert_element_type.61, bf16[1024,24,64]{0,2,1:T(8,128)(2,1)} %convert_element_type.62), kind=kOutput, calls=%fused_computation.3 | convolution fusion | flops 3296722944 | bytes 57671680 | tf_op jit(solution)/shard_map/thk,shk->hts/dot_general | solution.py:39
  65.5 21.4 %fusion.38 = f32[24,64,1024]{2,1,0:T(8,128)} fusion(bf16[1024,24,64]{0,2,1:T(8,128)(2,1)} %fusion.19, bf16[24,1024,1024]{2,1,0:T(8,128)(2,1)} %select_convert_fusion.1), kind=kOutput, calls=%fused_computation.58 | convolution fusion | flops 3221225472 | bytes 59768832 | tf_op jit(solution)/shard_map/hts,thv->shv/dot_general | solution.py:58
  86.9 24.1 %fusion.33 = f32[24,64,1024]{2,1,0:T(8,128)} fusion(bf16[1024,24,64]{0,2,1:T(8,128)(2,1)} %convert_element_type.60, bf16[24,1024,1024]{2,1,0:T(8,128)(2,1)} %select_convert_fusion.1), kind=kOutput, calls=%fused_computation.53 | convolution fusion | flops 3221225472 | bytes 59768832 | tf_op jit(solution)/shard_map/hts,shv->thv/dot_general | solution.py:44
  111.0 23.1 %select_convert_fusion = bf16[24,1024,1024]{2,1,0:T(8,128)(2,1)} fusion(pred[1024,1024]{1,0:T(8,128)(4,1)} %fusion.1, bf16[1024,24,64]{0,2,1:T(8,128)(2,1)} %fusion.19, bf16[1024,24,64]{0,2,1:T(8,128)(2,1)} %convert_element_type.60), kind=kOutput, calls=%fused_computation.2 | convolution fusion | flops 3296722944 | bytes 57671680 | tf_op jit(solution)/shard_map/thv,shv->hts/dot_general | solution.py:52
  134.1 21.4 %fusion.36 = f32[24,64,1024]{2,1,0:T(8,128)} fusion(bf16[1024,24,64]{0,2,1:T(8,128)(2,1)} %convert_element_type.61, bf16[24,1024,1024]{2,1,0:T(8,128)(2,1)} %select_convert_fusion), kind=kOutput, calls=%fused_computation.56 | convolution fusion | flops 3221225472 | bytes 59768832 | tf_op jit(solution)/shard_map/hts,thk->shk/dot_general | solution.py:56
  155.5 24.2 %fusion.34 = f32[24,64,1024]{2,1,0:T(8,128)} fusion(bf16[1024,24,64]{0,2,1:T(8,128)(2,1)} %convert_element_type.62, bf16[24,1024,1024]{2,1,0:T(8,128)(2,1)} %select_convert_fusion), kind=kOutput, calls=%fused_computation.54 | convolution fusion | flops 3221225472 | bytes 59768832 | tf_op jit(solution)/shard_map/hts,shk->thk/dot_general | solution.py:54
  181.7 4.8 fusion.15
  189.4 110.2 %while.20 = (s32[]{:T(128)}, f32[24,64,64]{2,1,0:T(8,128)}, f32[]{:T(128)}, f32[24,64,64]{2,1,0:T(8,128)}, s32[]{:T(128)}) while((s32[]{:T(128)}, f32[24,64,64]{2,1,0:T(8,128)}, f32[]{:T(128)}, f32[24,64,64]{2,1,0:T(8,128)}, s32[]{:T(128)}) %tuple.37), condition=%wide.region_5.6_spmd, body=%wide.region_4.5_spmd.sunk | while | flops 196610 | bytes 2752617 | solution.py:29
  191.8 4.6 collective-permute-start
  196.4 8.9 %collective-permute-done = f32[24,64,64]{2,1,0:T(8,128)} collective-permute-done((f32[24,64,64]{2,1,0:T(8,128)}, f32[24,64,64]{2,1,0:T(8,128)}, u32[]{:S(2)}, u32[]{:S(2)}) %collective-permute-start) | collective-permute-done | bytes 393248 | tf_op jit(solution)/shard_map/while/body/eval_jaxpr/ppermute | solution.py:28
  207.7 4.4 collective-permute-start
  212.1 8.9 %collective-permute-done = f32[24,64,64]{2,1,0:T(8,128)} collective-permute-done((f32[24,64,64]{2,1,0:T(8,128)}, f32[24,64,64]{2,1,0:T(8,128)}, u32[]{:S(2)}, u32[]{:S(2)}) %collective-permute-start) | collective-permute-done | bytes 393248 | tf_op jit(solution)/shard_map/while/body/eval_jaxpr/ppermute | solution.py:28
  223.4 4.4 collective-permute-start
  227.8 8.9 %collective-permute-done = f32[24,64,64]{2,1,0:T(8,128)} collective-permute-done((f32[24,64,64]{2,1,0:T(8,128)}, f32[24,64,64]{2,1,0:T(8,128)}, u32[]{:S(2)}, u32[]{:S(2)}) %collective-permute-start) | collective-permute-done | bytes 393248 | tf_op jit(solution)/shard_map/while/body/eval_jaxpr/ppermute | solution.py:28
  239.1 4.4 collective-permute-start
  243.6 8.9 %collective-permute-done = f32[24,64,64]{2,1,0:T(8,128)} collective-permute-done((f32[24,64,64]{2,1,0:T(8,128)}, f32[24,64,64]{2,1,0:T(8,128)}, u32[]{:S(2)}, u32[]{:S(2)}) %collective-permute-start) | collective-permute-done | bytes 393248 | tf_op jit(solution)/shard_map/while/body/eval_jaxpr/ppermute | solution.py:28
  254.8 4.4 collective-permute-start
  259.3 8.9 %collective-permute-done = f32[24,64,64]{2,1,0:T(8,128)} collective-permute-done((f32[24,64,64]{2,1,0:T(8,128)}, f32[24,64,64]{2,1,0:T(8,128)}, u32[]{:S(2)}, u32[]{:S(2)}) %collective-permute-start) | collective-permute-done | bytes 393248 | tf_op jit(solution)/shard_map/while/body/eval_jaxpr/ppermute | solution.py:28
  270.6 4.4 collective-permute-start
  275.0 8.9 %collective-permute-done = f32[24,64,64]{2,1,0:T(8,128)} collective-permute-done((f32[24,64,64]{2,1,0:T(8,128)}, f32[24,64,64]{2,1,0:T(8,128)}, u32[]{:S(2)}, u32[]{:S(2)}) %collective-permute-start) | collective-permute-done | bytes 393248 | tf_op jit(solution)/shard_map/while/body/eval_jaxpr/ppermute | solution.py:28
  286.3 4.4 collective-permute-start
  290.7 8.9 %collective-permute-done = f32[24,64,64]{2,1,0:T(8,128)} collective-permute-done((f32[24,64,64]{2,1,0:T(8,128)}, f32[24,64,64]{2,1,0:T(8,128)}, u32[]{:S(2)}, u32[]{:S(2)}) %collective-permute-start) | collective-permute-done | bytes 393248 | tf_op jit(solution)/shard_map/while/body/eval_jaxpr/ppermute | solution.py:28
  299.6 5.2 fusion.2
  304.8 7.7 fusion.9
  313.5 110.7 %while.21 = (s32[]{:T(128)}, f32[24,64,64]{2,1,0:T(8,128)}, f32[]{:T(128)}, f32[24,64,64]{2,1,0:T(8,128)}, s32[]{:T(128)}) while((s32[]{:T(128)}, f32[24,64,64]{2,1,0:T(8,128)}, f32[]{:T(128)}, f32[24,64,64]{2,1,0:T(8,128)}, s32[]{:T(128)}) %tuple.40), condition=%wide.region_7.8_spmd, body=%wide.region_6.7_spmd.sunk | while | flops 196610 | bytes 2752617 | solution.py:29
  317.8 12.1 %collective-permute-done.1 = f32[24,64,64]{2,1,0:T(8,128)} collective-permute-done((f32[24,64,64]{2,1,0:T(8,128)}, f32[24,64,64]{2,1,0:T(8,128)}, u32[]{:S(2)}, u32[]{:S(2)}) %collective-permute-start.1) | collective-permute-done | bytes 393248 | tf_op jit(solution)/shard_map/while/body/eval_jaxpr/ppermute | solution.py:28
  334.3 11.4 %collective-permute-done.1 = f32[24,64,64]{2,1,0:T(8,128)} collective-permute-done((f32[24,64,64]{2,1,0:T(8,128)}, f32[24,64,64]{2,1,0:T(8,128)}, u32[]{:S(2)}, u32[]{:S(2)}) %collective-permute-start.1) | collective-permute-done | bytes 393248 | tf_op jit(solution)/shard_map/while/body/eval_jaxpr/ppermute | solution.py:28
  350.0 11.4 %collective-permute-done.1 = f32[24,64,64]{2,1,0:T(8,128)} collective-permute-done((f32[24,64,64]{2,1,0:T(8,128)}, f32[24,64,64]{2,1,0:T(8,128)}, u32[]{:S(2)}, u32[]{:S(2)}) %collective-permute-start.1) | collective-permute-done | bytes 393248 | tf_op jit(solution)/shard_map/while/body/eval_jaxpr/ppermute | solution.py:28
  365.7 11.4 %collective-permute-done.1 = f32[24,64,64]{2,1,0:T(8,128)} collective-permute-done((f32[24,64,64]{2,1,0:T(8,128)}, f32[24,64,64]{2,1,0:T(8,128)}, u32[]{:S(2)}, u32[]{:S(2)}) %collective-permute-start.1) | collective-permute-done | bytes 393248 | tf_op jit(solution)/shard_map/while/body/eval_jaxpr/ppermute | solution.py:28
  381.4 11.4 %collective-permute-done.1 = f32[24,64,64]{2,1,0:T(8,128)} collective-permute-done((f32[24,64,64]{2,1,0:T(8,128)}, f32[24,64,64]{2,1,0:T(8,128)}, u32[]{:S(2)}, u32[]{:S(2)}) %collective-permute-start.1) | collective-permute-done | bytes 393248 | tf_op jit(solution)/shard_map/while/body/eval_jaxpr/ppermute | solution.py:28
  397.2 11.4 %collective-permute-done.1 = f32[24,64,64]{2,1,0:T(8,128)} collective-permute-done((f32[24,64,64]{2,1,0:T(8,128)}, f32[24,64,64]{2,1,0:T(8,128)}, u32[]{:S(2)}, u32[]{:S(2)}) %collective-permute-start.1) | collective-permute-done | bytes 393248 | tf_op jit(solution)/shard_map/while/body/eval_jaxpr/ppermute | solution.py:28
  412.9 11.4 %collective-permute-done.1 = f32[24,64,64]{2,1,0:T(8,128)} collective-permute-done((f32[24,64,64]{2,1,0:T(8,128)}, f32[24,64,64]{2,1,0:T(8,128)}, u32[]{:S(2)}, u32[]{:S(2)}) %collective-permute-start.1) | collective-permute-done | bytes 393248 | tf_op jit(solution)/shard_map/while/body/eval_jaxpr/ppermute | solution.py:28
  424.2 5.2 fusion.5
  431.1 7.5 convolution_bitcast_fusion
  444.1 7.5 convolution_bitcast_fusion.1
  451.7 7.7 convolution_bitcast_fusion.2
  459.5 9.4 %bitcast_convert_fusion = bf16[1024,1536]{1,0:T(8,128)(2,1)} fusion(bf16[1024,24,64]{0,2,1:T(8,128)(2,1)} %copy-done.5, bf16[24,64,1536]{2,1,0:T(8,128)(2,1)} %param.16), kind=kOutput, calls=%fused_computation.7 | convolution fusion | flops 4833411072 | bytes 11010048 | tf_op jit(solution)/shard_map/thk,hkc->tc/dot_general | solution.py:47
  468.9 7.4 fusion.37
  476.4 5.2 fusion.35
  481.6 7.3 fusion
  488.9 346.4 %all-reduce.3.cloned.1.call-done = (f32[1536,24,64]{0,2,1:T(8,128)}, f32[1536,24,64]{0,2,1:T(8,128)}, f32[1536,24,64]{0,2,1:T(8,128)}, f32[24,64,1536]{2,1,0:T(8,128)}) async-done(((f32[1536,24,64]{0,2,1:T(8,128)}, f32[1536,24,64]{0,2,1:T(8,128)}, f32[1536,24,64]{0,2,1:T(8,128)}, f32[24,64,1536]{2,1,0:T(8,128)}), (f32[1536,24,64]{0,2,1:T(8,128)}, f32[1536,24,64]{0,2,1:T(8,128)}, f32[1536,24,64]{0,2,1:T(8,128)}, ...) | async-done | bytes 37748752 | tf_op jit(solution)/shard_map/psum | solution.py:67
  835.4 8.7 %copy.36 = f32[1536,24,64]{0,2,1:T(8,128)} copy(f32[1536,24,64]{0,2,1:T(8,128)} %get-tuple-element.158) | data formatting | bytes 18874368
  844.1 8.9 %copy.37 = f32[1536,24,64]{0,2,1:T(8,128)} copy(f32[1536,24,64]{0,2,1:T(8,128)} %get-tuple-element.159) | data formatting | bytes 18874368
  853.0 8.8 %copy.38 = f32[1536,24,64]{0,2,1:T(8,128)} copy(f32[1536,24,64]{0,2,1:T(8,128)} %get-tuple-element.160) | data formatting | bytes 18874368
  (110 shorter events, 74.7 us)
Async XLA Ops:
  7.2 4.4 copy-start
  7.2 828.2 %all-reduce.3.cloned.1.call-start = ((), (), s32[]{:S(2)}) async-start(), calls=%async_computation | async-start | bytes 75497472 | tf_op jit(solution)/shard_map/psum | solution.py:67
  10.0 10.8 %slice-start.9 = ((s8[4718592]{0:T(1024)(128)(4,1)}), s8[4194304]{0:T(1024)(128)(4,1)S(1)}, s32[]{:S(2)}) async-start(s8[4718592]{0:T(1024)(128)(4,1)} %bitcast.98), calls=%async_computation.10 | async-start | bytes 8388608
  11.6 9.2 %slice-start.10 = ((s8[4718592]{0:T(1024)(128)(4,1)}), s8[524288]{0:T(1024)(128)(4,1)S(1)}, s32[]{:S(2)}) async-start(s8[4718592]{0:T(1024)(128)(4,1)} %bitcast.98), calls=%async_computation.11 | async-start | bytes 1048576
  18.6 9.5 %slice-start.11 = ((s8[4718592]{0:T(1024)(128)(4,1)}), s8[4194304]{0:T(1024)(128)(4,1)S(1)}, s32[]{:S(2)}) async-start(s8[4718592]{0:T(1024)(128)(4,1)} %bitcast.101), calls=%async_computation.12 | async-start | bytes 8388608
  20.8 7.3 slice-start.12
  25.9 9.5 %slice-start.7 = ((s8[4718592]{0:T(1024)(128)(4,1)}), s8[4194304]{0:T(1024)(128)(4,1)S(1)}, s32[]{:S(2)}) async-start(s8[4718592]{0:T(1024)(128)(4,1)} %bitcast.96), calls=%async_computation.8 | async-start | bytes 8388608
  28.1 7.3 slice-start.8
  33.2 2.9 copy-start.12
  181.6 4.9 copy-start.2
  181.7 4.9 copy-start.3
  191.8 13.5 %collective-permute-start = (f32[24,64,64]{2,1,0:T(8,128)}, f32[24,64,64]{2,1,0:T(8,128)}, u32[]{:S(2)}, u32[]{:S(2)}) collective-permute-start(f32[24,64,64]{2,1,0:T(8,128)} %multiply_add_fusion.4), channel_id=1, source_target_pairs={{0,1},{1,2},{2,3},{3,4},{4,5},{5,6},{6,7},{8,9},{9,10},{10,11},{11... | collective-permute-start | bytes 1179656 | tf_op jit(solution)/shard_map/while/body/eval_jaxpr/ppermute | solution.py:28
  207.7 13.3 %collective-permute-start = (f32[24,64,64]{2,1,0:T(8,128)}, f32[24,64,64]{2,1,0:T(8,128)}, u32[]{:S(2)}, u32[]{:S(2)}) collective-permute-start(f32[24,64,64]{2,1,0:T(8,128)} %multiply_add_fusion.4), channel_id=1, source_target_pairs={{0,1},{1,2},{2,3},{3,4},{4,5},{5,6},{6,7},{8,9},{9,10},{10,11},{11... | collective-permute-start | bytes 1179656 | tf_op jit(solution)/shard_map/while/body/eval_jaxpr/ppermute | solution.py:28
  223.4 13.3 %collective-permute-start = (f32[24,64,64]{2,1,0:T(8,128)}, f32[24,64,64]{2,1,0:T(8,128)}, u32[]{:S(2)}, u32[]{:S(2)}) collective-permute-start(f32[24,64,64]{2,1,0:T(8,128)} %multiply_add_fusion.4), channel_id=1, source_target_pairs={{0,1},{1,2},{2,3},{3,4},{4,5},{5,6},{6,7},{8,9},{9,10},{10,11},{11... | collective-permute-start | bytes 1179656 | tf_op jit(solution)/shard_map/while/body/eval_jaxpr/ppermute | solution.py:28
  239.1 13.3 %collective-permute-start = (f32[24,64,64]{2,1,0:T(8,128)}, f32[24,64,64]{2,1,0:T(8,128)}, u32[]{:S(2)}, u32[]{:S(2)}) collective-permute-start(f32[24,64,64]{2,1,0:T(8,128)} %multiply_add_fusion.4), channel_id=1, source_target_pairs={{0,1},{1,2},{2,3},{3,4},{4,5},{5,6},{6,7},{8,9},{9,10},{10,11},{11... | collective-permute-start | bytes 1179656 | tf_op jit(solution)/shard_map/while/body/eval_jaxpr/ppermute | solution.py:28
  254.8 13.3 %collective-permute-start = (f32[24,64,64]{2,1,0:T(8,128)}, f32[24,64,64]{2,1,0:T(8,128)}, u32[]{:S(2)}, u32[]{:S(2)}) collective-permute-start(f32[24,64,64]{2,1,0:T(8,128)} %multiply_add_fusion.4), channel_id=1, source_target_pairs={{0,1},{1,2},{2,3},{3,4},{4,5},{5,6},{6,7},{8,9},{9,10},{10,11},{11... | collective-permute-start | bytes 1179656 | tf_op jit(solution)/shard_map/while/body/eval_jaxpr/ppermute | solution.py:28
  270.6 13.3 %collective-permute-start = (f32[24,64,64]{2,1,0:T(8,128)}, f32[24,64,64]{2,1,0:T(8,128)}, u32[]{:S(2)}, u32[]{:S(2)}) collective-permute-start(f32[24,64,64]{2,1,0:T(8,128)} %multiply_add_fusion.4), channel_id=1, source_target_pairs={{0,1},{1,2},{2,3},{3,4},{4,5},{5,6},{6,7},{8,9},{9,10},{10,11},{11... | collective-permute-start | bytes 1179656 | tf_op jit(solution)/shard_map/while/body/eval_jaxpr/ppermute | solution.py:28
  286.3 13.3 %collective-permute-start = (f32[24,64,64]{2,1,0:T(8,128)}, f32[24,64,64]{2,1,0:T(8,128)}, u32[]{:S(2)}, u32[]{:S(2)}) collective-permute-start(f32[24,64,64]{2,1,0:T(8,128)} %multiply_add_fusion.4), channel_id=1, source_target_pairs={{0,1},{1,2},{2,3},{3,4},{4,5},{5,6},{6,7},{8,9},{9,10},{10,11},{11... | collective-permute-start | bytes 1179656 | tf_op jit(solution)/shard_map/while/body/eval_jaxpr/ppermute | solution.py:28
  299.6 5.2 copy-start.13
  304.8 7.7 copy-start.5
  315.9 14.1 %collective-permute-start.1 = (f32[24,64,64]{2,1,0:T(8,128)}, f32[24,64,64]{2,1,0:T(8,128)}, u32[]{:S(2)}, u32[]{:S(2)}) collective-permute-start(f32[24,64,64]{2,1,0:T(8,128)} %multiply_add_fusion.5), channel_id=1, source_target_pairs={{1,0},{2,1},{3,2},{4,3},{5,4},{6,5},{7,6},{9,8},{10,9},{11,10},{12... | collective-permute-start | bytes 1179656 | tf_op jit(solution)/shard_map/while/body/eval_jaxpr/ppermute | solution.py:28
  332.4 13.3 %collective-permute-start.1 = (f32[24,64,64]{2,1,0:T(8,128)}, f32[24,64,64]{2,1,0:T(8,128)}, u32[]{:S(2)}, u32[]{:S(2)}) collective-permute-start(f32[24,64,64]{2,1,0:T(8,128)} %multiply_add_fusion.5), channel_id=1, source_target_pairs={{1,0},{2,1},{3,2},{4,3},{5,4},{6,5},{7,6},{9,8},{10,9},{11,10},{12... | collective-permute-start | bytes 1179656 | tf_op jit(solution)/shard_map/while/body/eval_jaxpr/ppermute | solution.py:28
  348.1 13.3 %collective-permute-start.1 = (f32[24,64,64]{2,1,0:T(8,128)}, f32[24,64,64]{2,1,0:T(8,128)}, u32[]{:S(2)}, u32[]{:S(2)}) collective-permute-start(f32[24,64,64]{2,1,0:T(8,128)} %multiply_add_fusion.5), channel_id=1, source_target_pairs={{1,0},{2,1},{3,2},{4,3},{5,4},{6,5},{7,6},{9,8},{10,9},{11,10},{12... | collective-permute-start | bytes 1179656 | tf_op jit(solution)/shard_map/while/body/eval_jaxpr/ppermute | solution.py:28
  363.8 13.3 %collective-permute-start.1 = (f32[24,64,64]{2,1,0:T(8,128)}, f32[24,64,64]{2,1,0:T(8,128)}, u32[]{:S(2)}, u32[]{:S(2)}) collective-permute-start(f32[24,64,64]{2,1,0:T(8,128)} %multiply_add_fusion.5), channel_id=1, source_target_pairs={{1,0},{2,1},{3,2},{4,3},{5,4},{6,5},{7,6},{9,8},{10,9},{11,10},{12... | collective-permute-start | bytes 1179656 | tf_op jit(solution)/shard_map/while/body/eval_jaxpr/ppermute | solution.py:28
  379.5 13.3 %collective-permute-start.1 = (f32[24,64,64]{2,1,0:T(8,128)}, f32[24,64,64]{2,1,0:T(8,128)}, u32[]{:S(2)}, u32[]{:S(2)}) collective-permute-start(f32[24,64,64]{2,1,0:T(8,128)} %multiply_add_fusion.5), channel_id=1, source_target_pairs={{1,0},{2,1},{3,2},{4,3},{5,4},{6,5},{7,6},{9,8},{10,9},{11,10},{12... | collective-permute-start | bytes 1179656 | tf_op jit(solution)/shard_map/while/body/eval_jaxpr/ppermute | solution.py:28
  395.2 13.3 %collective-permute-start.1 = (f32[24,64,64]{2,1,0:T(8,128)}, f32[24,64,64]{2,1,0:T(8,128)}, u32[]{:S(2)}, u32[]{:S(2)}) collective-permute-start(f32[24,64,64]{2,1,0:T(8,128)} %multiply_add_fusion.5), channel_id=1, source_target_pairs={{1,0},{2,1},{3,2},{4,3},{5,4},{6,5},{7,6},{9,8},{10,9},{11,10},{12... | collective-permute-start | bytes 1179656 | tf_op jit(solution)/shard_map/while/body/eval_jaxpr/ppermute | solution.py:28
  410.9 13.3 %collective-permute-start.1 = (f32[24,64,64]{2,1,0:T(8,128)}, f32[24,64,64]{2,1,0:T(8,128)}, u32[]{:S(2)}, u32[]{:S(2)}) collective-permute-start(f32[24,64,64]{2,1,0:T(8,128)} %multiply_add_fusion.5), channel_id=1, source_target_pairs={{1,0},{2,1},{3,2},{4,3},{5,4},{6,5},{7,6},{9,8},{10,9},{11,10},{12... | collective-permute-start | bytes 1179656 | tf_op jit(solution)/shard_map/while/body/eval_jaxpr/ppermute | solution.py:28
  424.2 14.4 %slice-start.2 = ((s8[6291456]{0:T(1024)(128)(4,1)}), s8[4194304]{0:T(1024)(128)(4,1)S(1)}, s32[]{:S(2)}) async-start(s8[6291456]{0:T(1024)(128)(4,1)} %bitcast.88), calls=%async_computation.3 | async-start | bytes 8388608
  424.2 16.9 %slice-start = ((s8[6291456]{0:T(1024)(128)(4,1)}), s8[4194304]{0:T(1024)(128)(4,1)S(1)}, s32[]{:S(2)}) async-start(s8[6291456]{0:T(1024)(128)(4,1)} %bitcast.86), calls=%async_computation.1 | async-start | bytes 8388608
  429.4 1.7 copy-start.6
  431.1 7.5 slice-start.3
  431.1 7.5 copy-start.4
  431.1 10.1 %slice-start.1 = ((s8[6291456]{0:T(1024)(128)(4,1)}), s8[2097152]{0:T(1024)(128)(4,1)S(1)}, s32[]{:S(2)}) async-start(s8[6291456]{0:T(1024)(128)(4,1)} %bitcast.86), calls=%async_computation.2 | async-start | bytes 4194304
  438.7 2.5 copy-start.1
  441.2 10.5 %copy-start.8 = (bf16[1024,24,64]{0,2,1:T(8,128)(2,1)}, bf16[1024,24,64]{0,2,1:T(8,128)(2,1)S(1)}, u32[]{:S(2)}) copy-start(bf16[1024,24,64]{0,2,1:T(8,128)(2,1)S(1)} %fusion.3) | copy-start | bytes 9437188
  444.1 7.5 copy-start.10
  459.4 9.4 %copy-start.11 = (bf16[1024,24,64]{0,2,1:T(8,128)(2,1)S(1)}, bf16[1024,24,64]{0,2,1:T(8,128)(2,1)}, u32[]{:S(2)}) copy-start(bf16[1024,24,64]{0,2,1:T(8,128)(2,1)} %copy-done.10) | copy-start | bytes 9437188
  459.5 16.9 %slice-start.13 = ((s8[4718592]{0:T(1024)(128)(4,1)}), s8[4194304]{0:T(1024)(128)(4,1)S(1)}, s32[]{:S(2)}) async-start(s8[4718592]{0:T(1024)(128)(4,1)} %bitcast.104), calls=%async_computation.14 | async-start | bytes 8388608
  468.9 7.5 copy-start.9
  468.9 7.5 slice-start.14
  468.9 12.7 %slice-start.15 = ((s8[4718592]{0:T(1024)(128)(4,1)}), s8[4194304]{0:T(1024)(128)(4,1)S(1)}, s32[]{:S(2)}) async-start(s8[4718592]{0:T(1024)(128)(4,1)} %bitcast.107), calls=%async_computation.16 | async-start | bytes 8388608
  476.4 5.2 copy-start.7
  476.4 5.2 slice-start.16
  844.1 17.7 %slice-start.4 = ((s8[9437184]{0:T(1024)(128)(4,1)}), s8[4194304]{0:T(1024)(128)(4,1)S(1)}, s32[]{:S(2)}) async-start(s8[9437184]{0:T(1024)(128)(4,1)} %bitcast.90), calls=%async_computation.5 | async-start | bytes 8388608
  844.1 17.7 %slice-start.5 = ((s8[9437184]{0:T(1024)(128)(4,1)}), s8[4194304]{0:T(1024)(128)(4,1)S(1)}, s32[]{:S(2)}) async-start(s8[9437184]{0:T(1024)(128)(4,1)} %bitcast.90), calls=%async_computation.6 | async-start | bytes 8388608
  853.0 8.8 %slice-start.6 = ((s8[9437184]{0:T(1024)(128)(4,1)}), s8[1048576]{0:T(1024)(128)(4,1)S(1)}, s32[]{:S(2)}) async-start(s8[9437184]{0:T(1024)(128)(4,1)} %bitcast.90), calls=%async_computation.7 | async-start | bytes 2097152
Sparse Core Ops, SparseCore 0:
  459.6 375.7 all-reduce.2
where the time goes:
time: 882 us; the launch traced here: 873 us
  waiting for transfers between devices  489 us (55%)
  matrix products  243 us (28%)
  other arithmetic  45.2 us (5%)
  starting transfers between devices  44.8 us (5%)
  local copies, waits for them, and re-layouts  34.9 us (4%)
  between operations  15.5 us (2%)
    psum x1, waiting for transfers between devices, device_body(): dw_q, dw_k, dw_v, dw_o = lax.psum((dw_q, dw_k, dw_v, dw_o), 'sp')  346 us
    ppermute x14, waiting for transfers between devices, hop_step(): return lax.ppermute(doc_gate * hop_carry + local_state, 'sp', perm_list)  143 us
    ppermute x14, starting transfers between devices, hop_step(): return lax.ppermute(doc_gate * hop_carry + local_state, 'sp', perm_list)  44.8 us
    add x14, other arithmetic, hop_step(): return lax.ppermute(doc_gate * hop_carry + local_state, 'sp', perm_list)  33.4 us
    unnamed x66, local copies, waits for them, and re-layouts  32.8 us
    dot_general x1, matrix products, device_body(): jnp.einsum('hts,shk->thk', d_prob, k_rows, preferred_element_type=jnp.flo...  24.2 us
    dot_general x1, matrix products, device_body(): jnp.einsum('hts,shv->thv', attn_prob, v_rows, preferred_element_type=jnp....  24.1 us
    dot_general x1, matrix products, device_body(): jnp.einsum('thv,shv->hts', d_out, v_rows, preferred_element_type=jnp.floa...  23.1 us
  transfers between devices with their start and end apart: 15, of which 15 were waited for; matrix products, arithmetic and copies ran while one was open for 3% of the time, Pallas kernels for 0%

commit v1 on v0

v1 whole, which is shorter than its diff:
```python
import functools
import math
import jax
import jax.numpy as jnp
from jax import lax
from jax.experimental import pallas as pl
from jax.experimental.pallas import tpu as pltpu
from jax.sharding import PartitionSpec as P

MESH = pl.DeviceIdType.MESH
BF16 = jnp.bfloat16
F32 = jnp.float32
HEAD = 64
QUAD = 4 * HEAD
BLK = 256
VMEM_CAP = 64 * 1024 * 1024 - 128 * 1024

NN = (((1,), (0,)), ((), ()))
NT = (((1,), (1,)), ((), ()))
TN = (((0,), (0,)), ((), ()))


def mm(lhs, rhs, dims):
    return lax.dot_general(lhs, rhs, dims, preferred_element_type=F32)


def pack_states(full):
    lane = lax.broadcasted_iota(jnp.int32, (HEAD, 2 * HEAD), 1)
    first = jnp.where(lane < HEAD, full[0:HEAD, 0:2 * HEAD], full[HEAD:2 * HEAD, 0:2 * HEAD])
    second = jnp.where(lane < HEAD, full[2 * HEAD:3 * HEAD, 2 * HEAD:], full[3 * HEAD:, 2 * HEAD:])
    return jnp.concatenate([first, second], axis=0)


def spread_states(packed):
    lane = lax.broadcasted_iota(jnp.int32, (HEAD, 2 * HEAD), 1)
    zero = jnp.zeros((HEAD, 2 * HEAD), F32)
    rows = []
    for head in range(4):
        pair = packed[(head // 2) * HEAD:(head // 2 + 1) * HEAD, :]
        own = jnp.where((lane < HEAD) == (head % 2 == 0), pair, 0.0)
        rows.append(jnp.concatenate([own, zero] if head < 2 else [zero, own], axis=1))
    return jnp.concatenate(rows, axis=0)


def proj_kernel(flag_ref, x_ref, dy_ref, wq_ref, wk_ref, wv_ref, wo_ref,
                qt_ref, kt_ref, vt_ref, dot_ref, mt_ref, nt_ref, bound_ref):
    toks = x_ref.shape[0]

    @pl.when(pl.program_id(0) == 0)
    def _():
        lane = lax.broadcasted_iota(jnp.int32, (8, toks), 1)
        flags = jnp.broadcast_to(flag_ref[...], (8, toks))
        last = jnp.where(flags > 0, lane.astype(F32), -1.0)
        step = 1
        while step < toks:
            last = jnp.maximum(last, jnp.where(lane >= step, pltpu.roll(last, step, 1), -1.0))
            step *= 2
        bound_ref[...] = last

    bound = bound_ref[0:1, :]
    last_bound = jnp.max(bound, axis=1, keepdims=True)
    pos = lax.broadcasted_iota(jnp.int32, (1, toks), 1).astype(F32)
    head_row = bound < 0.0
    tail_row = pos >= last_bound
    x_val = x_ref[...]
    q_val = mm(wq_ref[...], x_val, NT).astype(BF16)
    qt_ref[...] = q_val
    k_val = mm(wk_ref[...], x_val, NT).astype(BF16)
    kt_ref[...] = k_val
    v_raw = mm(wv_ref[...], x_val, NT)
    vt_ref[...] = v_raw.astype(BF16)
    mt_ref[...] = pack_states(mm(jnp.where(tail_row, v_raw, 0.0).astype(BF16), k_val, NT))
    d_raw = mm(wo_ref[...], dy_ref[...], NT)
    dot_ref[...] = d_raw.astype(BF16)
    nt_ref[...] = pack_states(mm(jnp.where(head_row, d_raw, 0.0).astype(BF16), q_val, NT))


def project(flags, x_loc, dy_loc, wq, wk, wv, wo):
    toks, width = x_loc.shape
    steps = width // QUAD
    whole = lambda i: (0, 0)
    rows = lambda i: (i, 0)
    act = jax.ShapeDtypeStruct((width, toks), BF16)
    state = jax.ShapeDtypeStruct((width // 2, 2 * HEAD), F32)
    return pl.pallas_call(
        proj_kernel,
        name='project',
        grid=(steps,),
        in_specs=[pl.BlockSpec((1, toks), whole), pl.BlockSpec((toks, width), whole), pl.BlockSpec((toks, width), whole)]
        + [pl.BlockSpec((QUAD, width), rows)] * 4,
        out_specs=[pl.BlockSpec((QUAD, toks), rows)] * 4 + [pl.BlockSpec((QUAD // 2, 2 * HEAD), rows)] * 2
        + [pl.BlockSpec((8, toks), whole)],
        out_shape=[act] * 4 + [state] * 2 + [jax.ShapeDtypeStruct((8, toks), F32)],
        compiler_params=pltpu.CompilerParams(vmem_limit_bytes=VMEM_CAP),
        cost_estimate=pl.CostEstimate(flops=8 * toks * width * width, bytes_accessed=40 * 1024 * 1024, transcendentals=0),
    )(flags.reshape(1, toks), x_loc, dy_loc, wq, wk, wv, wo)


def attn_kernel(devs, scale, qt_ref, kt_ref, vt_ref, dot_ref, mt_ref, nt_ref, bound_ref,
                ot_ref, dvt_ref, dkt_ref, dqt_ref,
                acc_o, acc_q, acc_k, acc_v, s_in, r_in, s_out, r_out, stage, send_sem, recv_sem, out_sem):
    width, toks = qt_ref.shape
    heads = width // HEAD
    nblk = toks // BLK
    me = lax.axis_index('sp')
    barrier = pltpu.get_barrier_semaphore()

    for dev in (lax.rem(me + 1, devs), lax.rem(me + devs - 1, devs)):
        pl.semaphore_signal(barrier, inc=1, device_id={'sp': dev}, device_id_type=MESH)
    pl.semaphore_wait(barrier, 2)

    gate = jnp.where(jnp.max(bound_ref[0:1, :], axis=1, keepdims=True) < 0.0, 1.0, 0.0)
    fwd = pltpu.make_async_remote_copy(src_ref=s_out, dst_ref=s_in, send_sem=send_sem.at[0], recv_sem=recv_sem.at[0],
                                       device_id={'sp': jnp.minimum(me + 1, devs - 1)}, device_id_type=MESH)
    bwd = pltpu.make_async_remote_copy(src_ref=r_out, dst_ref=r_in, send_sem=send_sem.at[1], recv_sem=recv_sem.at[1],
                                       device_id={'sp': jnp.maximum(me - 1, 0)}, device_id_type=MESH)

    @pl.when(me == 0)
    def _():
        s_in[...] = jnp.zeros_like(s_in)
        s_out[...] = mt_ref[...]

    @pl.when(me == devs - 1)
    def _():
        r_in[...] = jnp.zeros_like(r_in)
        r_out[...] = nt_ref[...]

    @pl.when(me == 0)
    def _():
        fwd.start()

    @pl.when(me == devs - 1)
    def _():
        bwd.start()

    s_turn = jnp.maximum((me * heads) // devs - 1, 0)
    r_turn = jnp.maximum(((devs - 1 - me) * heads) // devs - 1, 0)

    def take_fwd():
        fwd.wait_recv()

        @pl.when(me < devs - 1)
        def _():
            s_out[...] = gate * s_in[...] + mt_ref[...]
            fwd.start()

    def take_bwd():
        bwd.wait_recv()

        @pl.when(me > 0)
        def _():
            r_out[...] = gate * r_in[...] + nt_ref[...]
            bwd.start()

    diag = (lax.broadcasted_iota(jnp.int32, (BLK, BLK), 0) <= lax.broadcasted_iota(jnp.int32, (BLK, BLK), 1))
    row_id = lax.broadcasted_iota(jnp.int32, (BLK, BLK), 0).astype(F32)

    def head_step(head, carry):
        base = pl.multiple_of(head * HEAD, HEAD)
        rows = pl.ds(base, HEAD)
        for tb in range(nblk):
            t_cols = pl.ds(tb * BLK, BLK)
            q_val = qt_ref[rows, t_cols]
            d_val = dot_ref[rows, t_cols]
            low = bound_ref[0:1, t_cols]
            o_sum = None
            q_sum = None
            for sb in range(tb + 1):
                s_cols = pl.ds(sb * BLK, BLK)
                k_val = kt_ref[rows, s_cols]
                v_val = vt_ref[rows, s_cols]
                seen = row_id + float(sb * BLK) >= low
                if sb == tb:
                    seen = jnp.logical_and(seen, diag)
                prob = jnp.where(seen, mm(k_val, q_val, TN) * scale, 0.0).astype(BF16)
                d_prob = jnp.where(seen, mm(v_val, d_val, TN) * scale, 0.0).astype(BF16)
                o_part = mm(v_val, prob, NN)
                q_part = mm(k_val, d_prob, NN)
                k_part = mm(q_val, d_prob, NT)
                v_part = mm(d_val, prob, NT)
                o_sum = o_part if o_sum is None else o_sum + o_part
                q_sum = q_part if q_sum is None else q_sum + q_part
                if sb == tb:
                    acc_k[rows, s_cols] = k_part
                    acc_v[rows, s_cols] = v_part
                else:
                    acc_k[rows, s_cols] += k_part
                    acc_v[rows, s_cols] += v_part
            acc_o[rows, t_cols] = o_sum
            acc_q[rows, t_cols] = q_sum
        early = me * 2 < devs

        @pl.when(jnp.logical_and(early, jnp.logical_and(me > 0, head == s_turn)))
        def _():
            take_fwd()

        @pl.when(jnp.logical_and(me < devs - 1, head == r_turn))
        def _():
            take_bwd()

        @pl.when(jnp.logical_and(jnp.logical_not(early), head == s_turn))
        def _():
            take_fwd()
        return carry

    lax.fori_loop(0, heads, head_step, 0)

    @pl.when(me < devs - 1)
    def _():
        fwd.wait_send()

    @pl.when(me > 0)
    def _():
        bwd.wait_send()

    bound = bound_ref[0:1, :]
    last_bound = jnp.max(bound, axis=1, keepdims=True)
    pos = lax.broadcasted_iota(jnp.int32, (1, toks), 1).astype(F32)
    head_row = jnp.where(bound < 0.0, scale, 0.0)
    tail_row = jnp.where(pos >= last_bound, scale, 0.0)
    outs = (ot_ref, dqt_ref, dvt_ref, dkt_ref)

    def out_copy(which, quad, slot):
        return pltpu.make_async_copy(stage.at[slot, which], outs[which].at[pl.ds(quad * QUAD, QUAD)], out_sem.at[slot, which])

    def quad_step(quad, carry):
        slot = lax.rem(quad, 2)

        @pl.when(quad >= 2)
        def _():
            for which in range(4):
                out_copy(which, quad - 2, slot).wait()
        rows = pl.ds(pl.multiple_of(quad * QUAD, QUAD), QUAD)
        packed = pl.ds(pl.multiple_of(quad * (QUAD // 2), QUAD // 2), QUAD // 2)
        s_full = spread_states(s_in[packed, :]).astype(BF16)
        r_full = spread_states(r_in[packed, :]).astype(BF16)
        for tb in range(nblk):
            cols = pl.ds(tb * BLK, BLK)
            h_row = head_row[:, tb * BLK:(tb + 1) * BLK]
            e_row = tail_row[:, tb * BLK:(tb + 1) * BLK]
            stage[slot, 0, :, cols] = (acc_o[rows, cols] + mm(s_full, qt_ref[rows, cols], NN) * h_row).astype(BF16)
            stage[slot, 1, :, cols] = (acc_q[rows, cols] + mm(s_full, dot_ref[rows, cols], TN) * h_row).astype(BF16)
            stage[slot, 2, :, cols] = (acc_v[rows, cols] + mm(r_full, kt_ref[rows, cols], NN) * e_row).astype(BF16)
            stage[slot, 3, :, cols] = (acc_k[rows, cols] + mm(r_full, vt_ref[rows, cols], TN) * e_row).astype(BF16)
        for which in range(4):
            out_copy(which, quad, slot).start()
        return carry

    quads = width // QUAD
    lax.fori_loop(0, quads, quad_step, 0)
    for quad in range(max(quads - 2, 0), quads):
        for which in range(4):
            out_copy(which, quad, quad % 2).wait()


def attend(devs, scale, qt, kt, vt, dot_t, mt, nt, bound):
    width, toks = qt.shape
    act = jax.ShapeDtypeStruct((width, toks), BF16)
    state = pltpu.VMEM(mt.shape, F32)
    return pl.pallas_call(
        functools.partial(attn_kernel, devs, scale),
        name='attend',
        in_specs=[pl.BlockSpec(memory_space=pltpu.VMEM)] * 7,
        out_specs=[pl.BlockSpec(memory_space=pl.ANY)] * 4,
        out_shape=[act] * 4,
        scratch_shapes=[pltpu.VMEM((width, toks), F32)] * 4 + [state] * 4
        + [pltpu.VMEM((2, 4, QUAD, toks), BF16), pltpu.SemaphoreType.DMA((2,)), pltpu.SemaphoreType.DMA((2,)),
           pltpu.SemaphoreType.DMA((2, 4))],
        compiler_params=pltpu.CompilerParams(vmem_limit_bytes=VMEM_CAP, collective_id=0, has_side_effects=True),
        cost_estimate=pl.CostEstimate(flops=12 * toks * toks * width, bytes_accessed=30 * 1024 * 1024, transcendentals=0),
    )(qt, kt, vt, dot_t, mt, nt, bound)


ACC_SLOTS = 8
MSG_SLOTS = 4


def ring_kernel(devs, seg, ot_ref, dvt_ref, dkt_ref, dqt_ref, x_ref, dy_ref, out_ref,
                xy, lhs, part, acc, inbox, xy_sem, lhs_sem, pair_send, pair_recv, rs_send, rs_recv,
                ag_send, ag_recv, fin_sem, peer_send, peer_recv):
    width, toks = ot_ref.shape
    chips = devs // 2
    per = width // seg
    count = 4 * per
    half = seg // 2
    side = seg // 4
    piece = side // chips
    me = lax.axis_index('sp')
    core = lax.rem(me, 2)
    chip = me // 2
    partner = chip * 2 + 1 - core
    targets = (lax.rem(chip + 1, chips) * 2 + core, lax.rem(chip + chips - 1, chips) * 2 + core)

    srcs = (ot_ref, dvt_ref, dkt_ref, dqt_ref)

    def lhs_copy(which, row, slot):
        return pltpu.make_async_copy(srcs[which].at[pl.ds(row, seg)], lhs.at[slot], lhs_sem.at[slot])

    def start_lhs(idx):
        for which in range(4):
            @pl.when(idx // per == which)
            def _():
                lhs_copy(which, pl.multiple_of(lax.rem(idx, per) * seg, seg), lax.rem(idx, 2)).start()

    load_dy = pltpu.make_async_copy(dy_ref, xy.at[0], xy_sem.at[0])
    load_x = pltpu.make_async_copy(x_ref, xy.at[1], xy_sem.at[1])
    load_dy.start()
    load_x.start()
    start_lhs(jnp.int32(0))

    barrier = pltpu.get_barrier_semaphore()
    for dev in (partner,) + targets:
        pl.semaphore_signal(barrier, inc=1, device_id={'sp': dev}, device_id_type=MESH)
    pl.semaphore_wait(barrier, 3)
    load_dy.wait()
    load_x.wait()

    def remote(src, dst, s_sem, r_sem, dev):
        return pltpu.make_async_remote_copy(src_ref=src, dst_ref=dst, send_sem=s_sem, recv_sem=r_sem,
                                            device_id={'sp': dev}, device_id_type=MESH)

    def ring_idx(idx):
        return lax.rem(idx + 4 * chips, chips)

    def pair_copy(idx):
        slot = lax.rem(idx, ACC_SLOTS)
        src = part.at[lax.rem(idx, 2), pl.ds(pl.multiple_of((1 - core) * half, half), half)]
        return remote(src, acc.at[slot], pair_send.at[slot], pair_recv.at[slot], partner)

    def acc_rows(idx, way, chunk):
        return acc.at[lax.rem(idx, ACC_SLOTS), pl.ds(pl.multiple_of(way * side + chunk * piece, piece), piece)]

    def out_rows(idx, owner, way, chunk):
        row = idx * seg + owner * half + way * side + chunk * piece
        return out_ref.at[pl.ds(pl.multiple_of(row, piece), piece)]

    def sent_chunk(way, step):
        return ring_idx(chip - step if way == 0 else chip + step)

    def rs_copy(idx, way, step):
        slot = lax.rem(idx, MSG_SLOTS)
        return remote(acc_rows(idx, way, sent_chunk(way, step)), inbox.at[way, step, slot],
                      rs_send.at[way, step, slot], rs_recv.at[way, step, slot], targets[way])

    def ag_chunk(way, step):
        return ring_idx(chip + 1 - step if way == 0 else chip - 1 + step)

    def ag_copy(idx, way, step):
        slot = lax.rem(idx, MSG_SLOTS)
        rows = out_rows(idx, core, way, ag_chunk(way, step))
        src = acc_rows(idx, way, ag_chunk(way, 0)) if step == 0 else rows
        return remote(src, rows, ag_send.at[way, step, slot], ag_recv.at[way, step, slot], targets[way])

    def fin_copy(idx, way):
        chunk = ag_chunk(way, 0)
        return pltpu.make_async_copy(acc_rows(idx, way, chunk), out_rows(idx, core, way, chunk),
                                     fin_sem.at[way, lax.rem(idx, MSG_SLOTS)])

    def peer_copy(idx, way, step):
        slot = lax.rem(idx, MSG_SLOTS)
        rows = out_rows(idx, core, way, ag_chunk(way, step))
        src = acc_rows(idx, way, ag_chunk(way, 0)) if step == 0 else rows
        return remote(src, rows, peer_send.at[way, step, slot], peer_recv.at[way, step, slot], partner)

    def stage_partial(idx):
        slot = lax.rem(idx, 2)
        lhs_copy(0, 0, slot).wait()

        @pl.when(idx + 1 < count)
        def _():
            start_lhs(idx + 1)
        rhs_id = jnp.minimum(idx // per, 1)
        tile_m = min(256, seg)
        tile_n = 512 if width % 512 == 0 else width

        def tile(step, carry):
            cols = pl.ds(pl.multiple_of(step * tile_n, tile_n), tile_n)
            for row in range(0, seg, tile_m):
                part[slot, row:row + tile_m, cols] = mm(lhs[slot, row:row + tile_m, :], xy[rhs_id, :, cols], NN)
            return carry
        lax.fori_loop(0, width // tile_n, tile, 0)
        pair_copy(idx).start()

    def add_rows(idx, way, step):
        chunk = sent_chunk(way, step)
        rows = pl.ds(pl.multiple_of(way * side + chunk * piece, piece), piece)
        slot = lax.rem(idx, ACC_SLOTS)
        acc[slot, rows, :] = acc[slot, rows, :] + inbox[way, step - 1, lax.rem(idx, MSG_SLOTS)]

    def stage_pair(idx):
        copy = pair_copy(idx)
        copy.wait()
        slot = lax.rem(idx, ACC_SLOTS)

        def add(step, carry):
            rows = pl.ds(pl.multiple_of(step * piece, piece), piece)
            own = pl.ds(pl.multiple_of(core * half + step * piece, piece), piece)
            acc[slot, rows, :] = acc[slot, rows, :] + part[lax.rem(idx, 2), own, :]
            return carry
        lax.fori_loop(0, half // piece, add, 0)
        for way in range(2):
            rs_copy(idx, way, 0).start()

    def stage_reduce(idx, step):
        for way in range(2):
            prev = rs_copy(idx, way, step - 1)
            prev.wait_send()
            prev.wait_recv()
            add_rows(idx, way, step)
            if step < chips - 1:
                rs_copy(idx, way, step).start()
            else:
                ag_copy(idx, way, 0).start()
                peer_copy(idx, way, 0).start()
                fin_copy(idx, way).start()

    def stage_gather(idx, step):
        for way in range(2):
            ag_copy(idx, way, step).wait_send()
            slot = lax.rem(idx, MSG_SLOTS)
            got = out_rows(idx, core, way, ag_chunk(way, step + 1))
            remote(got, got, ag_send.at[way, step, slot], ag_recv.at[way, step, slot], targets[way]).wait_recv()
            if step + 1 < chips - 1:
                ag_copy(idx, way, step + 1).start()
            peer_copy(idx, way, step + 1).start()
            if step == 0:
                fin_copy(idx, way).wait()
            finish_peer(idx, way, step)

    def finish_peer(idx, way, step):
        peer_copy(idx, way, step).wait_send()
        slot = lax.rem(idx, MSG_SLOTS)
        got = out_rows(idx, 1 - core, way, ag_chunk(way, step))
        remote(got, got, peer_send.at[way, step, slot], peer_recv.at[way, step, slot], partner).wait_recv()

    def stage_last(idx):
        for way in range(2):
            finish_peer(idx, way, chips - 1)

    stages = [stage_partial]
    order = [(2 * chips, stage_last)]
    for step in reversed(range(chips - 1)):
        order.append((chips + 1 + step, functools.partial(stage_gather, step=step)))
    for step in reversed(range(1, chips)):
        order.append((1 + step, functools.partial(stage_reduce, step=step)))
    order.append((1, stage_pair))
    order.insert(0, (0, stage_partial))

    def round_step(rnd, carry):
        for delay, stage in order:
            idx = rnd - delay

            @pl.when(jnp.logical_and(idx >= 0, idx < count))
            def _():
                stage(idx)
        return carry

    lax.fori_loop(0, count + 2 * chips, round_step, 0)


def ring_sum(devs, seg, ot, dvt, dkt, dqt, x_loc, dy_loc):
    width, toks = ot.shape
    chips = devs // 2
    piece = seg // 4 // chips
    dma = pltpu.SemaphoreType.DMA
    return pl.pallas_call(
        functools.partial(ring_kernel, devs, seg),
        name='ring_sum',
        in_specs=[pl.BlockSpec(memory_space=pl.ANY)] * 6,
        out_specs=pl.BlockSpec(memory_space=pl.ANY),
        out_shape=jax.ShapeDtypeStruct((4 * width, width), F32),
        scratch_shapes=[
            pltpu.VMEM((2, toks, width), BF16),
            pltpu.VMEM((2, seg, toks), BF16),
            pltpu.VMEM((2, seg, width), F32),
            pltpu.VMEM((ACC_SLOTS, seg // 2, width), F32),
            pltpu.VMEM((2, chips - 1, MSG_SLOTS, piece, width), F32),
            dma((2,)), dma((2,)), dma((ACC_SLOTS,)), dma((ACC_SLOTS,)),
            dma((2, chips - 1, MSG_SLOTS)), dma((2, chips - 1, MSG_SLOTS)),
            dma((2, chips - 1, MSG_SLOTS)), dma((2, chips - 1, MSG_SLOTS)),
            dma((2, MSG_SLOTS)),
            dma((2, chips, MSG_SLOTS)), dma((2, chips, MSG_SLOTS)),
        ],
        compiler_params=pltpu.CompilerParams(vmem_limit_bytes=VMEM_CAP, collective_id=1, has_side_effects=True),
        cost_estimate=pl.CostEstimate(flops=8 * toks * width * width, bytes_accessed=100 * 1024 * 1024, transcendentals=0),
    )(ot, dvt, dkt, dqt, x_loc, dy_loc)


def solution(mesh):
    devs = mesh.shape['sp']

    def device_body(x_loc, flag_loc, w_q, w_k, w_v, w_o, dy_loc):
        toks, width = x_loc.shape
        heads, head_dim = w_q.shape[1], w_q.shape[2]
        scale = 1.0 / (math.sqrt(head_dim) * toks)
        wq, wk, wv = [jnp.transpose(w, (1, 2, 0)).reshape(width, width) for w in (w_q, w_k, w_v)]
        wo = w_o.reshape(width, width)
        qt, kt, vt, dot_t, mt, nt, bound = project(flag_loc, x_loc, dy_loc, wq, wk, wv, wo)
        ot, dvt, dkt, dqt = attend(devs, scale, qt, kt, vt, dot_t, mt, nt, bound)
        y_loc = mm(ot, wo, TN).astype(BF16)
        dx_loc = (mm(dqt, wq, TN) + mm(dkt, wk, TN) + mm(dvt, wv, TN)).astype(BF16)
        seg = width // 3 if width % 3 == 0 else width // 2
        total = ring_sum(devs, seg, ot, dvt, dkt, dqt, x_loc, dy_loc)
        dw_o, dw_v, dw_k, dw_q = [total[i * width:(i + 1) * width].reshape(heads, head_dim, width) for i in range(4)]
        dw_q, dw_k, dw_v = [jnp.transpose(dw, (2, 0, 1)) for dw in (dw_q, dw_k, dw_v)]
        return y_loc, dx_loc, dw_q, dw_k, dw_v, dw_o

    row_spec = P(('dp', 'sp'), None)
    flag_spec = P(('dp', 'sp'))
    w_spec = P(None, None, None)
    dw_spec = P('dp', None, None)
    return jax.shard_map(device_body, mesh=mesh,
                         in_specs=(row_spec, flag_spec, w_spec, w_spec, w_spec, w_spec, row_spec),
                         out_specs=(row_spec, row_spec, dw_spec, dw_spec, dw_spec, dw_spec),
                         check_vma=False)
```

time: 882 us -> 492 us (0.56); the launches traced: 873 us -> 492 us
  waiting for transfers between devices: 489 us -> 0 us
  Pallas kernels: 0 us -> 438 us
  matrix products: 243 us -> 27.1 us
  other arithmetic: 45.2 us -> 0.01 us
  starting transfers between devices: 44.8 us -> 0 us
  between operations: 15.5 us -> 0.79 us
  local copies, waits for them, and re-layouts: 34.9 us -> 25.5 us
    pallas_call x0 -> x3, Pallas kernels: none -> 438 us  [the longest x1 321 us: ring_sum(): pl.pallas_call(functools.partial(ring_kernel, devs, seg), name='ring_sum'...]
    psum x1 -> x0, waiting for transfers between devices: 346 us -> none  [device_body(): dw_q, dw_k, dw_v, dw_o = lax.psum((dw_q, dw_k, dw_v, dw_o), 'sp')]
    dot_general x21 -> x4, matrix products: 226 us -> 27.1 us  [mm(): return lax.dot_general(lhs, rhs, dims, preferred_element_type=F32)]
    ppermute x14 -> x0, waiting for transfers between devices: 143 us -> none  [hop_step(): return lax.ppermute(doc_gate * hop_carry + local_state, 'sp', perm_list)]
    ppermute x14 -> x0, starting transfers between devices: 44.8 us -> none  [hop_step(): return lax.ppermute(doc_gate * hop_carry + local_state, 'sp', perm_list)]
    add x14 -> x0, other arithmetic: 33.4 us -> none  [hop_step(): return lax.ppermute(doc_gate * hop_carry + local_state, 'sp', perm_list)]
    unnamed x66 -> x16, local copies, waits for them, and re-layouts: 32.8 us -> 0.05 us
    slice x1, local copies, waits for them, and re-layouts: 0.07 us -> 25.4 us  [device_body(): total[i * width:(i + 1) * width].reshape(heads, head_dim, width)]
  transfers between devices with their start and end apart: 15 -> 0, of which waited for: 15 -> 0; matrix products, arithmetic and copies ran while one was open for 3% -> 0% of each run, Pallas kernels for 0% -> 0%
where the time goes in v1:
time: 492 us
  Pallas kernels  438 us (89%)
  matrix products  27.1 us (6%)
  local copies, waits for them, and re-layouts  25.5 us (5%)
    pallas_call x1, Pallas kernels, ring_sum(): pl.pallas_call(functools.partial(ring_kernel, devs, seg), name='ring_sum'...  321 us
    pallas_call x1, Pallas kernels, attend(): pl.pallas_call(functools.partial(attn_kernel, devs, scale), name='attend'...  88.9 us
    pallas_call x1, Pallas kernels, project(): pl.pallas_call(proj_kernel, name='project', grid=(steps,), in_specs=[pl.B...  28.9 us
    dot_general x4, matrix products, mm(): return lax.dot_general(lhs, rhs, dims, preferred_element_type=F32)  27.1 us
    slice x1, local copies, waits for them, and re-layouts, device_body(): total[i * width:(i + 1) * width].reshape(heads, head_dim, width)  25.4 us

profile of v1, /device:TPU:81, one launch (start us, length us, event | category | flops | bytes accessed | tf_op | source)
XLA Modules:
  0.0 491.8 jit_solution(10914344065986232688)
XLA Ops:
  0.6 28.9 %project.1 = (bf16[1536,1024]{1,0:T(8,128)(2,1)}, bf16[1536,1024]{1,0:T(8,128)(2,1)}, bf16[1536,1024]{1,0:T(8,128)(2,1)}, bf16[1536,1024]{1,0:T(8,128)(2,1)}, f3...) custom-call(s32[1,1024]{1,0:T(1,128)} %bitcast.45, bf16[1024,1536]{1,0:T(8,128)(2,1)} %x_ref.3, ...), custom_call_target="tpu_custom_call" | custom-call | flops 19327352832 | bytes 41943040 | tf_op jit(solution)/shard_map/project/pallas_call | solution.py:85
  29.5 88.9 %attend.1 = (bf16[1536,1024]{1,0:T(8,128)(2,1)}, bf16[1536,1024]{1,0:T(8,128)(2,1)}, bf16[1536,1024]{1,0:T(8,128)(2,1)}, bf16[1536,1024]{1,0:T(8,128)(2,1)}) custom-call(bf16[1536,1024]{1,0:T(8,128)(2,1)} %get-tuple-element.17.qt_ref, bf16[1536,1024]{1,0:T(8,128)(2,1)} %get-tuple-element.18.kt_ref, bf16[1536,1024]{1,0:T(8,128)(2,1)} %get-tuple-element.19.vt_ref, ...), custom_call_target="tpu_custom_call" | custom-call | flops 19327352832 | bytes 31457280 | tf_op jit(solution)/shard_map/attend/pallas_call | solution.py:260
  118.4 0.0 copy-start
  118.4 0.0 copy-start.2
  118.5 0.0 slice-start
  118.5 9.4 %convolution_convert_fusion = bf16[1024,1536]{1,0:T(8,128)(2,1)} fusion(bf16[1536,1024]{1,0:T(8,128)(2,1)} %get-tuple-element.24.ot_ref, bf16[1536,1536]{1,0:T(8,128)(2,1)} %bitcast.34), kind=kOutput, calls=%fused_computation.1 | convolution fusion | flops 4833411072 | bytes 11010048 | tf_op jit(solution)/shard_map/dot_general | solution.py:24
  127.9 0.0 copy-done
  127.9 0.0 copy-done.2
  127.9 0.0 slice-start.1
  127.9 0.0 copy-start.1
  127.9 0.0 slice-start.2
  127.9 5.2 %fusion.1 = f32[1024,1536]{1,0:T(8,128)S(1)} fusion(bf16[1536,1024]{1,0:T(8,128)(2,1)S(1)} %copy-done.2, bf16[1536,1536]{1,0:T(8,128)(2,1)S(1)} %bitcast.36), kind=kOutput, calls=%fused_computation.3 | convolution fusion | flops 4831838208 | bytes 14155776 | tf_op jit(solution)/shard_map/dot_general | solution.py:24
  133.1 0.0 slice-done
  133.1 0.0 slice-done.1
  133.1 0.0 copy-done.1
  133.1 0.0 slice-start.3
  133.2 0.0 copy-start.3
  133.2 5.2 %fusion.2 = f32[1024,1536]{1,0:T(8,128)S(1)} fusion(bf16[1536,1024]{1,0:T(8,128)(2,1)S(1)} %copy-done.1, bf16[1536,1536]{1,0:T(8,128)(2,1)S(1)} %bitcast.40), kind=kOutput, calls=%fused_computation.4 | convolution fusion | flops 4831838208 | bytes 14155776 | tf_op jit(solution)/shard_map/dot_general | solution.py:24
  138.4 0.0 slice-done.2
  138.4 0.0 slice-done.3
  138.4 0.0 copy-done.3
  138.4 7.3 %add_convert_fusion = bf16[1024,1536]{1,0:T(8,128)(2,1)} fusion(f32[1024,1536]{1,0:T(8,128)S(1)} %fusion.1, f32[1024,1536]{1,0:T(8,128)S(1)} %fusion.2, bf16[1536,1024]{1,0:T(8,128)(2,1)S(1)} %copy-done.3, bf16[1536,1536]{1,0:T(8,128)(2,1)S(1)} %bitcast.44), kind=kOutput, calls=%fused_computation | convolution fusion | flops 4836556800 | bytes 23592960 | tf_op jit(solution)/shard_map/dot_general | solution.py:24
  145.7 320.7 %ring_sum.1 = f32[6144,1536]{1,0:T(8,128)} custom-call(bf16[1536,1024]{1,0:T(8,128)(2,1)} %get-tuple-element.24.ot_ref, bf16[1536,1024]{1,0:T(8,128)(2,1)} %get-tuple-element.27.dvt_ref, bf16[1536,1024]{1,0:T(8,128)(2,1)} %get-tuple-element.26.dkt_ref, bf16[1536,1024]{1,0:T(8,128)(2,1)} %get-tuple-element.25.dqt_ref, bf16[1024,1536]{1,0:T(8,128)(2,1)} %x_ref.3, ...), custom_call_target="tpu_custom_call" | custom-call | flops 19327352832 | bytes 104857600 | tf_op jit(solution)/shard_map/ring_sum/pallas_call | solution.py:466
  466.4 25.4 %fusion = (f32[1536,1536]{1,0:T(8,128)}, f32[1536,1536]{1,0:T(8,128)}, f32[1536,1536]{1,0:T(8,128)}, f32[1536,1536]{1,0:T(8,128)}) fusion(f32[6144,1536]{1,0:T(8,128)} %ring_sum.1), kind=kLoop, calls=%fused_computation.2 | loop fusion | bytes 75497472 | tf_op jit(solution)/shard_map/slice | solution.py:504
  (2 shorter events, 0.0 us)
Async XLA Ops:
  118.4 9.5 %copy-start = (bf16[1536,24,64]{0,2,1:T(8,128)(2,1)S(1)}, bf16[1536,24,64]{0,2,1:T(8,128)(2,1)}, u32[]{:S(2)}) copy-start(bf16[1536,24,64]{0,2,1:T(8,128)(2,1)} %param.9) | copy-start | bytes 14155780
  118.4 9.4 %copy-start.2 = (bf16[1536,1024]{1,0:T(8,128)(2,1)S(1)}, bf16[1536,1024]{1,0:T(8,128)(2,1)}, u32[]{:S(2)}) copy-start(bf16[1536,1024]{1,0:T(8,128)(2,1)} %get-tuple-element.25.dqt_ref) | copy-start | bytes 9437188
  118.5 14.7 %slice-start = ((s8[4718592]{0:T(1024)(128)(4,1)}), s8[4194304]{0:T(1024)(128)(4,1)S(1)}, s32[]{:S(2)}) async-start(s8[4718592]{0:T(1024)(128)(4,1)} %bitcast.38), calls=%async_computation | async-start | bytes 8388608
  127.9 5.2 %slice-start.1 = ((s8[4718592]{0:T(1024)(128)(4,1)}), s8[524288]{0:T(1024)(128)(4,1)S(1)}, s32[]{:S(2)}) async-start(s8[4718592]{0:T(1024)(128)(4,1)} %bitcast.38), calls=%async_computation.1 | async-start | bytes 1048576
  127.9 5.2 %copy-start.1 = (bf16[1536,1024]{1,0:T(8,128)(2,1)S(1)}, bf16[1536,1024]{1,0:T(8,128)(2,1)}, u32[]{:S(2)}) copy-start(bf16[1536,1024]{1,0:T(8,128)(2,1)} %get-tuple-element.26.dkt_ref) | copy-start | bytes 9437188
  127.9 10.5 %slice-start.2 = ((s8[4718592]{0:T(1024)(128)(4,1)}), s8[4194304]{0:T(1024)(128)(4,1)S(1)}, s32[]{:S(2)}) async-start(s8[4718592]{0:T(1024)(128)(4,1)} %bitcast.42), calls=%async_computation.2 | async-start | bytes 8388608
  133.1 5.2 %slice-start.3 = ((s8[4718592]{0:T(1024)(128)(4,1)}), s8[524288]{0:T(1024)(128)(4,1)S(1)}, s32[]{:S(2)}) async-start(s8[4718592]{0:T(1024)(128)(4,1)} %bitcast.42), calls=%async_computation.3 | async-start | bytes 1048576
  133.2 5.2 %copy-start.3 = (bf16[1536,1024]{1,0:T(8,128)(2,1)S(1)}, bf16[1536,1024]{1,0:T(8,128)(2,1)}, u32[]{:S(2)}) copy-start(bf16[1536,1024]{1,0:T(8,128)(2,1)} %get-tuple-element.27.dvt_ref) | copy-start | bytes 9437188

commit v2 on v0

v2 whole, which is shorter than its diff:
```python
import functools
import math
import jax
import jax.numpy as jnp
from jax import lax
from jax.experimental import pallas as pl
from jax.experimental.pallas import tpu as pltpu
from jax.sharding import PartitionSpec as P

MESH = pl.DeviceIdType.MESH
BF16 = jnp.bfloat16
F32 = jnp.float32
HEAD = 64
QUAD = 4 * HEAD
BLK = 256
VMEM_CAP = 64 * 1024 * 1024 - 128 * 1024
ACC_SLOTS = 8
MSG_SLOTS = 4

NN = (((1,), (0,)), ((), ()))
NT = (((1,), (1,)), ((), ()))
TN = (((0,), (0,)), ((), ()))


def mm(lhs, rhs, dims):
    return lax.dot_general(lhs, rhs, dims, preferred_element_type=F32)


def pack_states(full):
    lane = lax.broadcasted_iota(jnp.int32, (HEAD, 2 * HEAD), 1)
    first = jnp.where(lane < HEAD, full[0:HEAD, 0:2 * HEAD], full[HEAD:2 * HEAD, 0:2 * HEAD])
    second = jnp.where(lane < HEAD, full[2 * HEAD:3 * HEAD, 2 * HEAD:], full[3 * HEAD:, 2 * HEAD:])
    return jnp.concatenate([first, second], axis=0)


def spread_states(packed):
    lane = lax.broadcasted_iota(jnp.int32, (HEAD, 2 * HEAD), 1)
    zero = jnp.zeros((HEAD, 2 * HEAD), F32)
    rows = []
    for head in range(4):
        pair = packed[(head // 2) * HEAD:(head // 2 + 1) * HEAD, :]
        own = jnp.where((lane < HEAD) == (head % 2 == 0), pair, 0.0)
        rows.append(jnp.concatenate([own, zero] if head < 2 else [zero, own], axis=1))
    return jnp.concatenate(rows, axis=0)


def fused_kernel(devs, scale, flag_ref, x_ref, dy_ref, wq_ref, wk_ref, wv_ref, wo_ref,
                 out_ref, ot_ref, dqt_ref, dvt_ref, dkt_ref,
                 xy, wbuf, qt, kt, vt, dt, mt, nt, s_in, r_in, s_out, r_out, bound_ref, raw, lhs, part, acc, inbox,
                 xy_sem, w_sem, act_sem, chain_send, chain_recv, pair_send, pair_recv, rs_send, rs_recv,
                 ag_send, ag_recv, fin_sem, peer_send, peer_recv):
    width, toks = qt.shape
    nquad = width // QUAD
    nblk = toks // BLK
    seg = QUAD
    count = 4 * nquad
    chips = devs // 2
    half = seg // 2
    side = seg // 4
    piece = side // chips
    me = lax.axis_index('sp')
    core = lax.rem(me, 2)
    chip = me // 2
    partner = chip * 2 + 1 - core
    targets = (lax.rem(chip + 1, chips) * 2 + core, lax.rem(chip + chips - 1, chips) * 2 + core)
    up = lax.rem(me + 1, devs)
    down = lax.rem(me + devs - 1, devs)

    load_x = pltpu.make_async_copy(x_ref, xy.at[1], xy_sem.at[1])
    load_dy = pltpu.make_async_copy(dy_ref, xy.at[0], xy_sem.at[0])
    load_x.start()

    def w_copies(tick, kv):
        slot = lax.rem(tick, 2)
        rows = pl.ds(pl.multiple_of(lax.rem(tick, nquad) * QUAD, QUAD), QUAD)
        pair = (wk_ref, wv_ref) if kv else (wq_ref, wo_ref)
        return [pltpu.make_async_copy(ref.at[rows], wbuf.at[slot, i], w_sem.at[slot, i]) for i, ref in enumerate(pair)]

    def start_w(tick):
        @pl.when(tick < nquad)
        def _():
            for copy in w_copies(tick, True):
                copy.start()

        @pl.when(jnp.logical_and(tick >= nquad, tick < 2 * nquad))
        def _():
            for copy in w_copies(tick, False):
                copy.start()

    start_w(jnp.int32(0))
    load_dy.start()

    barrier = pltpu.get_barrier_semaphore()
    for dev in (up, down, partner) + targets:
        pl.semaphore_signal(barrier, inc=1, device_id={'sp': dev}, device_id_type=MESH)

    lane = lax.broadcasted_iota(jnp.int32, (8, toks), 1)
    last = jnp.where(jnp.broadcast_to(flag_ref[...], (8, toks)) > 0, lane.astype(F32), -1.0)
    step = 1
    while step < toks:
        last = jnp.maximum(last, jnp.where(lane >= step, pltpu.roll(last, step, 1), -1.0))
        step *= 2
    bound_ref[...] = last
    bound = bound_ref[0:1, :]
    last_bound = jnp.max(bound, axis=1, keepdims=True)
    pos = lax.broadcasted_iota(jnp.int32, (1, toks), 1).astype(F32)
    gate = jnp.where(last_bound < 0.0, 1.0, 0.0)
    diag = (lax.broadcasted_iota(jnp.int32, (BLK, BLK), 0) <= lax.broadcasted_iota(jnp.int32, (BLK, BLK), 1))
    row_id = lax.broadcasted_iota(jnp.int32, (BLK, BLK), 0).astype(F32)

    pl.semaphore_wait(barrier, 5)
    load_x.wait()

    def quad_rows(quad):
        return pl.ds(pl.multiple_of(quad * QUAD, QUAD), QUAD)

    def pack_rows(quad):
        return pl.ds(pl.multiple_of(quad * (QUAD // 2), QUAD // 2), QUAD // 2)

    def project_kv(tick):
        slot = lax.rem(tick, 2)
        for copy in w_copies(tick, True):
            copy.wait()
        start_w(tick + 1)
        x_val = xy[1]
        k_val = mm(wbuf[slot, 0], x_val, NT).astype(BF16)
        kt[quad_rows(tick), :] = k_val
        v_raw = mm(wbuf[slot, 1], x_val, NT)
        vt[quad_rows(tick), :] = v_raw.astype(BF16)
        tail = pos >= last_bound
        mt[pack_rows(tick), :] = pack_states(mm(jnp.where(tail, v_raw, 0.0).astype(BF16), k_val, NT))

    def project_qd(tick):
        slot = lax.rem(tick, 2)
        quad = tick - nquad
        for copy in w_copies(tick, False):
            copy.wait()
        start_w(tick + 1)

        @pl.when(quad == 0)
        def _():
            load_dy.wait()
        q_val = mm(wbuf[slot, 0], xy[1], NT).astype(BF16)
        qt[quad_rows(quad), :] = q_val
        d_raw = mm(wbuf[slot, 1], xy[0], NT)
        dt[quad_rows(quad), :] = d_raw.astype(BF16)
        nt[pack_rows(quad), :] = pack_states(mm(jnp.where(bound < 0.0, d_raw, 0.0).astype(BF16), q_val, NT))

    def chain_copy(way, quad):
        rows = pack_rows(quad)
        src, dst, dev = ((s_out, s_in, up), (r_out, r_in, down))[way]
        return pltpu.make_async_remote_copy(src_ref=src.at[rows], dst_ref=dst.at[rows], send_sem=chain_send.at[way, quad],
                                            recv_sem=chain_recv.at[way, quad], device_id={'sp': dev}, device_id_type=MESH)

    def chain_step(way, quad, first, final):
        rows = pack_rows(quad)
        own, got, nxt = ((mt, s_in, s_out), (nt, r_in, r_out))[way]

        @pl.when(first)
        def _():
            got[rows, :] = jnp.zeros((QUAD // 2, 2 * HEAD), F32)

        @pl.when(jnp.logical_not(first))
        def _():
            chain_copy(way, quad).wait_recv()

        @pl.when(jnp.logical_not(final))
        def _():
            nxt[rows, :] = gate * got[rows, :] + own[rows, :]
            chain_copy(way, quad).start()

    def remote(src, dst, s_sem, r_sem, dev):
        return pltpu.make_async_remote_copy(src_ref=src, dst_ref=dst, send_sem=s_sem, recv_sem=r_sem,
                                            device_id={'sp': dev}, device_id_type=MESH)

    def ring_idx(idx):
        return lax.rem(idx + 4 * chips, chips)

    def pair_copy(idx):
        slot = lax.rem(idx, ACC_SLOTS)
        src = part.at[lax.rem(idx, 2), pl.ds(pl.multiple_of((1 - core) * half, half), half)]
        return remote(src, acc.at[slot], pair_send.at[slot], pair_recv.at[slot], partner)

    def acc_rows(idx, way, chunk):
        return acc.at[lax.rem(idx, ACC_SLOTS), pl.ds(pl.multiple_of(way * side + chunk * piece, piece), piece)]

    def out_rows(idx, owner, way, chunk):
        row = idx * seg + owner * half + way * side + chunk * piece
        return out_ref.at[pl.ds(pl.multiple_of(row, piece), piece)]

    def sent_chunk(way, step):
        return ring_idx(chip - step if way == 0 else chip + step)

    def rs_copy(idx, way, step):
        slot = lax.rem(idx, MSG_SLOTS)
        return remote(acc_rows(idx, way, sent_chunk(way, step)), inbox.at[way, step, slot],
                      rs_send.at[way, step, slot], rs_recv.at[way, step, slot], targets[way])

    def ag_chunk(way, step):
        return ring_idx(chip + 1 - step if way == 0 else chip - 1 + step)

    def ag_copy(idx, way, step):
        slot = lax.rem(idx, MSG_SLOTS)
        rows = out_rows(idx, core, way, ag_chunk(way, step))
        src = acc_rows(idx, way, ag_chunk(way, 0)) if step == 0 else rows
        return remote(src, rows, ag_send.at[way, step, slot], ag_recv.at[way, step, slot], targets[way])

    def fin_copy(idx, way):
        chunk = ag_chunk(way, 0)
        return pltpu.make_async_copy(acc_rows(idx, way, chunk), out_rows(idx, core, way, chunk),
                                     fin_sem.at[way, lax.rem(idx, MSG_SLOTS)])

    def peer_copy(idx, way, step):
        slot = lax.rem(idx, MSG_SLOTS)
        rows = out_rows(idx, core, way, ag_chunk(way, step))
        src = acc_rows(idx, way, ag_chunk(way, 0)) if step == 0 else rows
        return remote(src, rows, peer_send.at[way, step, slot], peer_recv.at[way, step, slot], partner)


    acts = (ot_ref, dqt_ref, dvt_ref, dkt_ref)

    def act_copy(idx, kind):
        slot = lax.rem(idx, 2)
        return pltpu.make_async_copy(lhs.at[slot], acts[kind].at[quad_rows(lax.rem(idx, nquad))], act_sem.at[slot])

    def unit(idx, kind):
        quad = lax.rem(idx, nquad)
        slot = lax.rem(idx, 2)
        by_query = kind < 2
        left, right = (kt, qt) if kind % 2 == 0 else (vt, dt)
        value = (vt, kt, dt, qt)[kind]

        def head_step(head, carry):
            rows = pl.ds(pl.multiple_of(quad * QUAD + head * HEAD, HEAD), HEAD)
            for ob in range(nblk):
                total = None
                for ib in (range(ob + 1) if by_query else range(ob, nblk)):
                    tb, sb = (ob, ib) if by_query else (ib, ob)
                    t_cols, s_cols = pl.ds(tb * BLK, BLK), pl.ds(sb * BLK, BLK)
                    seen = row_id + float(sb * BLK) >= bound_ref[0:1, t_cols]
                    if sb == tb:
                        seen = jnp.logical_and(seen, diag)
                    prob = jnp.where(seen, mm(left[rows, s_cols], right[rows, t_cols], TN) * scale, 0.0).astype(BF16)
                    if by_query:
                        part_sum = mm(value[rows, s_cols], prob, NN)
                    else:
                        part_sum = mm(value[rows, t_cols], prob, NT)
                    total = part_sum if total is None else total + part_sum
                raw[pl.ds(pl.multiple_of(head * HEAD, HEAD), HEAD), ob * BLK:(ob + 1) * BLK] = total
            return carry

        lax.fori_loop(0, QUAD // HEAD, head_step, 0)
        state = s_in if by_query else r_in
        full = spread_states(state[pack_rows(quad), :]).astype(BF16)
        other = (qt, dt, kt, vt)[kind]
        dims = NN if kind % 2 == 0 else TN
        weight = jnp.where(bound < 0.0, scale, 0.0) if by_query else jnp.where(pos >= last_bound, scale, 0.0)
        for tb in range(nblk):
            cols = pl.ds(tb * BLK, BLK)
            extra = mm(full, other[quad_rows(quad), cols], dims) * weight[:, tb * BLK:(tb + 1) * BLK]
            lhs[slot, :, cols] = (raw[:, cols] + extra).astype(BF16)
        act_copy(idx, kind).start()

    def stage_partial(idx):
        slot = lax.rem(idx, 2)

        @pl.when(idx >= 2)
        def _():
            act_copy(idx, 0).wait()
        for kind in range(4):
            @pl.when(idx // nquad == kind)
            def _():
                unit(idx, kind)
        rhs_id = jnp.minimum(idx // nquad, 1)
        tile_n = 512 if width % 512 == 0 else width

        def tile(step, carry):
            cols = pl.ds(pl.multiple_of(step * tile_n, tile_n), tile_n)
            part[slot, :, cols] = mm(lhs[slot], xy[rhs_id, :, cols], NN)
            return carry
        lax.fori_loop(0, width // tile_n, tile, 0)
        pair_copy(idx).start()

    def add_rows(idx, way, step):
        chunk = sent_chunk(way, step)
        rows = pl.ds(pl.multiple_of(way * side + chunk * piece, piece), piece)
        slot = lax.rem(idx, ACC_SLOTS)
        acc[slot, rows, :] = acc[slot, rows, :] + inbox[way, step - 1, lax.rem(idx, MSG_SLOTS)]

    def stage_pair(idx):
        copy = pair_copy(idx)
        copy.wait()
        slot = lax.rem(idx, ACC_SLOTS)

        def add(step, carry):
            rows = pl.ds(pl.multiple_of(step * piece, piece), piece)
            own = pl.ds(pl.multiple_of(core * half + step * piece, piece), piece)
            acc[slot, rows, :] = acc[slot, rows, :] + part[lax.rem(idx, 2), own, :]
            return carry
        lax.fori_loop(0, half // piece, add, 0)
        for way in range(2):
            rs_copy(idx, way, 0).start()

    def stage_reduce(idx, step):
        for way in range(2):
            prev = rs_copy(idx, way, step - 1)
            prev.wait_send()
            prev.wait_recv()
            add_rows(idx, way, step)
            if step < chips - 1:
                rs_copy(idx, way, step).start()
            else:
                ag_copy(idx, way, 0).start()
                peer_copy(idx, way, 0).start()
                fin_copy(idx, way).start()

    def stage_gather(idx, step):
        for way in range(2):
            ag_copy(idx, way, step).wait_send()
            slot = lax.rem(idx, MSG_SLOTS)
            got = out_rows(idx, core, way, ag_chunk(way, step + 1))
            remote(got, got, ag_send.at[way, step, slot], ag_recv.at[way, step, slot], targets[way]).wait_recv()
            if step + 1 < chips - 1:
                ag_copy(idx, way, step + 1).start()
            peer_copy(idx, way, step + 1).start()
            if step == 0:
                fin_copy(idx, way).wait()
            finish_peer(idx, way, step)

    def finish_peer(idx, way, step):
        peer_copy(idx, way, step).wait_send()
        slot = lax.rem(idx, MSG_SLOTS)
        got = out_rows(idx, 1 - core, way, ag_chunk(way, step))
        remote(got, got, peer_send.at[way, step, slot], peer_recv.at[way, step, slot], partner).wait_recv()

    def stage_last(idx):
        for way in range(2):
            finish_peer(idx, way, chips - 1)

    order = [(2 * chips, stage_last)]
    for step in reversed(range(chips - 1)):
        order.append((chips + 1 + step, functools.partial(stage_gather, step=step)))
    for step in reversed(range(1, chips)):
        order.append((1 + step, functools.partial(stage_reduce, step=step)))
    order.append((1, stage_pair))
    order.append((0, stage_partial))
    lead = max(devs - 1, nquad)

    def tick_step(tick, carry):
        @pl.when(tick < nquad)
        def _():
            project_kv(tick)

        @pl.when(jnp.logical_and(tick >= nquad, tick < 2 * nquad))
        def _():
            project_qd(tick)
        s_quad = tick - me
        r_quad = tick - nquad - (devs - 1 - me)

        @pl.when(jnp.logical_and(s_quad >= 0, s_quad < nquad))
        def _():
            chain_step(0, s_quad, me == 0, me == devs - 1)

        @pl.when(jnp.logical_and(r_quad >= 0, r_quad < nquad))
        def _():
            chain_step(1, r_quad, me == devs - 1, me == 0)
        for delay, stage in order:
            idx = tick - lead - delay

            @pl.when(jnp.logical_and(idx >= 0, idx < count))
            def _():
                stage(idx)
        return carry

    lax.fori_loop(0, lead + count + 2 * chips, tick_step, 0)
    for idx in range(count - 2, count):
        act_copy(jnp.int32(idx), 3).wait()

    def chain_end(quad, carry):
        @pl.when(me < devs - 1)
        def _():
            chain_copy(0, quad).wait_send()

        @pl.when(me > 0)
        def _():
            chain_copy(1, quad).wait_send()
        return carry
    lax.fori_loop(0, nquad, chain_end, 0)


def fused(devs, scale, flags, x_loc, dy_loc, wq, wk, wv, wo):
    toks, width = x_loc.shape
    chips = devs // 2
    nquad = width // QUAD
    piece = QUAD // 4 // chips
    dma = pltpu.SemaphoreType.DMA
    act = jax.ShapeDtypeStruct((width, toks), BF16)
    state = pltpu.VMEM((width // 2, 2 * HEAD), F32)
    ring = (2, chips - 1, MSG_SLOTS)
    return pl.pallas_call(
        functools.partial(fused_kernel, devs, scale),
        name='fused',
        in_specs=[pl.BlockSpec(memory_space=pltpu.VMEM)] + [pl.BlockSpec(memory_space=pl.ANY)] * 6,
        out_specs=[pl.BlockSpec(memory_space=pl.ANY)] * 5,
        out_shape=[jax.ShapeDtypeStruct((4 * width, width), F32)] + [act] * 4,
        scratch_shapes=[
            pltpu.VMEM((2, toks, width), BF16),
            pltpu.VMEM((2, 2, QUAD, width), BF16),
            *[pltpu.VMEM((width, toks), BF16)] * 4,
            *[state] * 6,
            pltpu.VMEM((8, toks), F32),
            pltpu.VMEM((QUAD, toks), F32),
            pltpu.VMEM((2, QUAD, toks), BF16),
            pltpu.VMEM((2, QUAD, width), F32),
            pltpu.VMEM((ACC_SLOTS, QUAD // 2, width), F32),
            pltpu.VMEM((2, chips - 1, MSG_SLOTS, piece, width), F32),
            dma((2,)), dma((2, 2)), dma((2,)), dma((2, nquad)), dma((2, nquad)), dma((ACC_SLOTS,)), dma((ACC_SLOTS,)),
            dma(ring), dma(ring), dma(ring), dma(ring), dma((2, MSG_SLOTS)),
            dma((2, chips, MSG_SLOTS)), dma((2, chips, MSG_SLOTS)),
        ],
        compiler_params=pltpu.CompilerParams(vmem_limit_bytes=VMEM_CAP, collective_id=0, has_side_effects=True),
        cost_estimate=pl.CostEstimate(flops=24 * toks * width * width, bytes_accessed=150 * 1024 * 1024, transcendentals=0),
    )(flags.reshape(1, toks), x_loc, dy_loc, wq, wk, wv, wo)


def solution(mesh):
    devs = mesh.shape['sp']

    def device_body(x_loc, flag_loc, w_q, w_k, w_v, w_o, dy_loc):
        toks, width = x_loc.shape
        heads, head_dim = w_q.shape[1], w_q.shape[2]
        scale = 1.0 / (math.sqrt(head_dim) * toks)
        wq, wk, wv = [jnp.transpose(w, (1, 2, 0)).reshape(width, width) for w in (w_q, w_k, w_v)]
        wo = w_o.reshape(width, width)
        total, ot, dqt, dvt, dkt = fused(devs, scale, flag_loc, x_loc, dy_loc, wq, wk, wv, wo)
        y_loc = mm(ot, wo, TN).astype(BF16)
        dx_loc = (mm(dqt, wq, TN) + mm(dkt, wk, TN) + mm(dvt, wv, TN)).astype(BF16)
        dw_o, dw_q, dw_v, dw_k = [total[i * width:(i + 1) * width].reshape(heads, head_dim, width) for i in range(4)]
        dw_q, dw_k, dw_v = [jnp.transpose(dw, (2, 0, 1)) for dw in (dw_q, dw_k, dw_v)]
        return y_loc, dx_loc, dw_q, dw_k, dw_v, dw_o

    row_spec = P(('dp', 'sp'), None)
    flag_spec = P(('dp', 'sp'))
    w_spec = P(None, None, None)
    dw_spec = P('dp', None, None)
    return jax.shard_map(device_body, mesh=mesh,
                         in_specs=(row_spec, flag_spec, w_spec, w_spec, w_spec, w_spec, row_spec),
                         out_specs=(row_spec, row_spec, dw_spec, dw_spec, dw_spec, dw_spec),
                         check_vma=False)
```

time: 882 us -> 414 us (0.47); the launches traced: 873 us -> 414 us
  waiting for transfers between devices: 489 us -> 0 us
  Pallas kernels: 0 us -> 361 us
  matrix products: 243 us -> 27.1 us
  other arithmetic: 45.2 us -> 0.01 us
  starting transfers between devices: 44.8 us -> 0 us
  between operations: 15.5 us -> 0.78 us
  local copies, waits for them, and re-layouts: 34.9 us -> 25.5 us
    pallas_call x0 -> x1, Pallas kernels: none -> 361 us  [fused(): pl.pallas_call(functools.partial(fused_kernel, devs, scale), name='fused'...]
    psum x1 -> x0, waiting for transfers between devices: 346 us -> none  [device_body(): dw_q, dw_k, dw_v, dw_o = lax.psum((dw_q, dw_k, dw_v, dw_o), 'sp')]
    dot_general x21 -> x4, matrix products: 226 us -> 27.1 us  [mm(): return lax.dot_general(lhs, rhs, dims, preferred_element_type=F32)]
    ppermute x14 -> x0, waiting for transfers between devices: 143 us -> none  [hop_step(): return lax.ppermute(doc_gate * hop_carry + local_state, 'sp', perm_list)]
    ppermute x14 -> x0, starting transfers between devices: 44.8 us -> none  [hop_step(): return lax.ppermute(doc_gate * hop_carry + local_state, 'sp', perm_list)]
    add x14 -> x0, other arithmetic: 33.4 us -> none  [hop_step(): return lax.ppermute(doc_gate * hop_carry + local_state, 'sp', perm_list)]
    unnamed x66 -> x16, local copies, waits for them, and re-layouts: 32.8 us -> 0.05 us
    slice x1, local copies, waits for them, and re-layouts: 0.07 us -> 25.4 us  [device_body(): total[i * width:(i + 1) * width].reshape(heads, head_dim, width)]
  transfers between devices with their start and end apart: 15 -> 0, of which waited for: 15 -> 0; matrix products, arithmetic and copies ran while one was open for 3% -> 0% of each run, Pallas kernels for 0% -> 0%
where the time goes in v2:
time: 414 us
  Pallas kernels  361 us (87%)
  matrix products  27.1 us (7%)
  local copies, waits for them, and re-layouts  25.5 us (6%)
    pallas_call x1, Pallas kernels, fused(): pl.pallas_call(functools.partial(fused_kernel, devs, scale), name='fused'...  361 us
    dot_general x4, matrix products, mm(): return lax.dot_general(lhs, rhs, dims, preferred_element_type=F32)  27.1 us
    slice x1, local copies, waits for them, and re-layouts, device_body(): total[i * width:(i + 1) * width].reshape(heads, head_dim, width)  25.4 us

profile of v2, /device:TPU:81, one launch (start us, length us, event | category | flops | bytes accessed | tf_op | source)
XLA Modules:
  0.0 414.2 jit_solution(3266077997108231587)
XLA Ops:
  0.6 360.9 %fused.1 = (f32[6144,1536]{1,0:T(8,128)}, bf16[1536,1024]{1,0:T(8,128)(2,1)}, bf16[1536,1024]{1,0:T(8,128)(2,1)}, bf16[1536,1024]{1,0:T(8,128)(2,1)}, bf16[1536,1024]{1,0:T(8,128)(2,1)}) custom-call(s32[1,1024]{1,0:T(1,128)} %bitcast.45, bf16[1024,1536]{1,0:T(8,128)(2,1)} %x_ref.1, bf16[1024,1536]{1,0:T(8,128)(2,1)} %dy_ref.1, bf16[1536,1536]{1,0:T(8,128)(2,1)} %bitcast.35, ...), custom_call_target="tpu_custom_call" | custom-call | flops 57982058496 | bytes 157286400 | tf_op jit(solution)/shard_map/fused/pallas_call | solution.py:400
  361.5 0.0 copy-start
  361.6 0.0 copy-start.2
  361.6 0.0 slice-start
  361.6 9.4 %convolution_convert_fusion = bf16[1024,1536]{1,0:T(8,128)(2,1)} fusion(bf16[1536,1024]{1,0:T(8,128)(2,1)} %get-tuple-element.11, bf16[1536,1536]{1,0:T(8,128)(2,1)} %bitcast.34), kind=kOutput, calls=%fused_computation.1 | convolution fusion | flops 4833411072 | bytes 11010048 | tf_op jit(solution)/shard_map/dot_general | solution.py:26
  371.0 0.0 copy-done
  371.0 0.0 copy-done.2
  371.0 0.0 slice-start.1
  371.0 0.0 copy-start.1
  371.0 0.0 slice-start.2
  371.0 5.2 %fusion.1 = f32[1024,1536]{1,0:T(8,128)S(1)} fusion(bf16[1536,1024]{1,0:T(8,128)(2,1)S(1)} %copy-done.2, bf16[1536,1536]{1,0:T(8,128)(2,1)S(1)} %bitcast.36), kind=kOutput, calls=%fused_computation.3 | convolution fusion | flops 4831838208 | bytes 14155776 | tf_op jit(solution)/shard_map/dot_general | solution.py:26
  376.2 0.0 slice-done
  376.2 0.0 slice-done.1
  376.2 0.0 copy-done.1
  376.3 0.0 slice-start.3
  376.3 0.0 copy-start.3
  376.3 5.2 %fusion.2 = f32[1024,1536]{1,0:T(8,128)S(1)} fusion(bf16[1536,1024]{1,0:T(8,128)(2,1)S(1)} %copy-done.1, bf16[1536,1536]{1,0:T(8,128)(2,1)S(1)} %bitcast.40), kind=kOutput, calls=%fused_computation.4 | convolution fusion | flops 4831838208 | bytes 14155776 | tf_op jit(solution)/shard_map/dot_general | solution.py:26
  381.5 0.0 slice-done.2
  381.5 0.0 slice-done.3
  381.5 0.0 copy-done.3
  381.5 7.3 %add_convert_fusion = bf16[1024,1536]{1,0:T(8,128)(2,1)} fusion(f32[1024,1536]{1,0:T(8,128)S(1)} %fusion.1, f32[1024,1536]{1,0:T(8,128)S(1)} %fusion.2, bf16[1536,1024]{1,0:T(8,128)(2,1)S(1)} %copy-done.3, bf16[1536,1536]{1,0:T(8,128)(2,1)S(1)} %bitcast.44), kind=kOutput, calls=%fused_computation | convolution fusion | flops 4836556800 | bytes 23592960 | tf_op jit(solution)/shard_map/dot_general | solution.py:26
  388.8 25.4 %fusion = (f32[1536,1536]{1,0:T(8,128)}, f32[1536,1536]{1,0:T(8,128)}, f32[1536,1536]{1,0:T(8,128)}, f32[1536,1536]{1,0:T(8,128)}) fusion(f32[6144,1536]{1,0:T(8,128)} %get-tuple-element.15), kind=kLoop, calls=%fused_computation.2 | loop fusion | bytes 75497472 | tf_op jit(solution)/shard_map/slice | solution.py:438
  (2 shorter events, 0.0 us)
Async XLA Ops:
  361.5 9.5 %copy-start = (bf16[1536,24,64]{0,2,1:T(8,128)(2,1)S(1)}, bf16[1536,24,64]{0,2,1:T(8,128)(2,1)}, u32[]{:S(2)}) copy-start(bf16[1536,24,64]{0,2,1:T(8,128)(2,1)} %param.9) | copy-start | bytes 14155780
  361.6 9.4 %copy-start.2 = (bf16[1536,1024]{1,0:T(8,128)(2,1)S(1)}, bf16[1536,1024]{1,0:T(8,128)(2,1)}, u32[]{:S(2)}) copy-start(bf16[1536,1024]{1,0:T(8,128)(2,1)} %get-tuple-element.12) | copy-start | bytes 9437188
  361.6 14.7 %slice-start = ((s8[4718592]{0:T(1024)(128)(4,1)}), s8[4194304]{0:T(1024)(128)(4,1)S(1)}, s32[]{:S(2)}) async-start(s8[4718592]{0:T(1024)(128)(4,1)} %bitcast.38), calls=%async_computation | async-start | bytes 8388608
  371.0 5.2 %slice-start.1 = ((s8[4718592]{0:T(1024)(128)(4,1)}), s8[524288]{0:T(1024)(128)(4,1)S(1)}, s32[]{:S(2)}) async-start(s8[4718592]{0:T(1024)(128)(4,1)} %bitcast.38), calls=%async_computation.1 | async-start | bytes 1048576
  371.0 5.2 %copy-start.1 = (bf16[1536,1024]{1,0:T(8,128)(2,1)S(1)}, bf16[1536,1024]{1,0:T(8,128)(2,1)}, u32[]{:S(2)}) copy-start(bf16[1536,1024]{1,0:T(8,128)(2,1)} %get-tuple-element.13) | copy-start | bytes 9437188
  371.0 10.5 %slice-start.2 = ((s8[4718592]{0:T(1024)(128)(4,1)}), s8[4194304]{0:T(1024)(128)(4,1)S(1)}, s32[]{:S(2)}) async-start(s8[4718592]{0:T(1024)(128)(4,1)} %bitcast.42), calls=%async_computation.2 | async-start | bytes 8388608
  376.3 5.2 %slice-start.3 = ((s8[4718592]{0:T(1024)(128)(4,1)}), s8[524288]{0:T(1024)(128)(4,1)S(1)}, s32[]{:S(2)}) async-start(s8[4718592]{0:T(1024)(128)(4,1)} %bitcast.42), calls=%async_computation.3 | async-start | bytes 1048576
  376.3 5.2 %copy-start.3 = (bf16[1536,1024]{1,0:T(8,128)(2,1)S(1)}, bf16[1536,1024]{1,0:T(8,128)(2,1)}, u32[]{:S(2)}) copy-start(bf16[1536,1024]{1,0:T(8,128)(2,1)} %get-tuple-element.14) | copy-start | bytes 9437188

commit v3 on v2

--- a/solution.py
+++ b/solution.py
@@ -45,9 +45,9 @@
 
 
 def fused_kernel(devs, scale, flag_ref, x_ref, dy_ref, wq_ref, wk_ref, wv_ref, wo_ref,
-                 out_ref, ot_ref, dqt_ref, dvt_ref, dkt_ref,
-                 xy, wbuf, qt, kt, vt, dt, mt, nt, s_in, r_in, s_out, r_out, bound_ref, raw, lhs, part, acc, inbox,
-                 xy_sem, w_sem, act_sem, chain_send, chain_recv, pair_send, pair_recv, rs_send, rs_recv,
+                 out_ref, y_ref, dx_ref,
+                 xy, wbuf, qt, kt, vt, dt, mt, nt, s_in, r_in, s_out, r_out, bound_ref, raw, lhs, ot, part, acc, inbox, y_acc, dx_acc, row_out,
+                 xy_sem, w_sem, row_sem, chain_send, chain_recv, pair_send, pair_recv, rs_send, rs_recv,
                  ag_send, ag_recv, fin_sem, peer_send, peer_recv):
     width, toks = qt.shape
     nquad = width // QUAD
@@ -217,11 +217,74 @@
         return remote(src, rows, peer_send.at[way, step, slot], peer_recv.at[way, step, slot], partner)
 
 
-    acts = (ot_ref, dqt_ref, dvt_ref, dkt_ref)
-
-    def act_copy(idx, kind):
+    def post_copies(idx):
         slot = lax.rem(idx, 2)
-        return pltpu.make_async_copy(lhs.at[slot], acts[kind].at[quad_rows(lax.rem(idx, nquad))], act_sem.at[slot])
+        rows = quad_rows(lax.rem(idx, nquad))
+        y_copy = pltpu.make_async_copy(wo_ref.at[rows], wbuf.at[slot, 1], w_sem.at[slot, 1])
+        return [pltpu.make_async_copy(ref.at[rows], wbuf.at[slot, 0], w_sem.at[slot, 0]) for ref in (wq_ref, wv_ref, wk_ref)], y_copy
+
+    def start_post(idx):
+        dx_copies, y_copy = post_copies(idx)
+        for kind in range(1, 4):
+            @pl.when(idx // nquad == kind)
+            def _():
+                dx_copies[kind - 1].start()
+
+        @pl.when(idx // nquad == 2)
+        def _():
+            y_copy.start()
+
+    def accumulate(total, rows_t, weight, fresh):
+        tile_t = 256
+
+        def tile(step, carry):
+            toks_at = pl.ds(pl.multiple_of(step * tile_t, tile_t), tile_t)
+            add = mm(rows_t[:, toks_at], weight[...], TN)
+
+            @pl.when(fresh)
+            def _():
+                total[toks_at, :] = add
+
+            @pl.when(jnp.logical_not(fresh))
+            def _():
+                total[toks_at, :] += add
+            return carry
+        lax.fori_loop(0, toks // tile_t, tile, 0)
+
+    def write_rows(total, dst):
+        tile_t = row_out.shape[1]
+        for i in range(toks // tile_t):
+            copy = pltpu.make_async_copy(row_out.at[i % 2], dst.at[i * tile_t:(i + 1) * tile_t], row_sem.at[i % 2])
+            if i >= 2:
+                copy.wait()
+            row_out[i % 2] = total[i * tile_t:(i + 1) * tile_t, :].astype(BF16)
+            copy.start()
+        for i in range(2):
+            pltpu.make_async_copy(row_out.at[i], dst.at[i * tile_t:(i + 1) * tile_t], row_sem.at[i]).wait()
+
+    def stage_post(idx):
+        slot = lax.rem(idx, 2)
+        kind = idx // nquad
+        dx_copies, y_copy = post_copies(idx)
+        dx_copies[0].wait()
+
+        @pl.when(idx + 1 < count)
+        def _():
+            start_post(idx + 1)
+        accumulate(dx_acc, lhs.at[slot], wbuf.at[slot, 0], idx == nquad)
+
+        @pl.when(kind == 2)
+        def _():
+            y_copy.wait()
+            accumulate(y_acc, ot.at[quad_rows(lax.rem(idx, nquad))], wbuf.at[slot, 1], idx == 2 * nquad)
+
+        @pl.when(idx == 3 * nquad)
+        def _():
+            write_rows(y_acc, y_ref)
+
+        @pl.when(idx == count - 1)
+        def _():
+            write_rows(dx_acc, dx_ref)
 
     def unit(idx, kind):
         quad = lax.rem(idx, nquad)
@@ -259,14 +322,11 @@
             cols = pl.ds(tb * BLK, BLK)
             extra = mm(full, other[quad_rows(quad), cols], dims) * weight[:, tb * BLK:(tb + 1) * BLK]
             lhs[slot, :, cols] = (raw[:, cols] + extra).astype(BF16)
-        act_copy(idx, kind).start()
+            if kind == 0:
+                ot[quad_rows(quad), cols] = lhs[slot, :, cols]
 
     def stage_partial(idx):
         slot = lax.rem(idx, 2)
-
-        @pl.when(idx >= 2)
-        def _():
-            act_copy(idx, 0).wait()
         for kind in range(4):
             @pl.when(idx // nquad == kind)
             def _():
@@ -280,6 +340,14 @@
             return carry
         lax.fori_loop(0, width // tile_n, tile, 0)
         pair_copy(idx).start()
+
+        @pl.when(idx == nquad - 1)
+        def _():
+            start_post(idx + 1)
+
+        @pl.when(idx >= nquad)
+        def _():
+            stage_post(idx)
 
     def add_rows(idx, way, step):
         chunk = sent_chunk(way, step)
@@ -373,8 +441,6 @@
         return carry
 
     lax.fori_loop(0, lead + count + 2 * chips, tick_step, 0)
-    for idx in range(count - 2, count):
-        act_copy(jnp.int32(idx), 3).wait()
 
     def chain_end(quad, carry):
         @pl.when(me < devs - 1)
@@ -394,15 +460,15 @@
     nquad = width // QUAD
     piece = QUAD // 4 // chips
     dma = pltpu.SemaphoreType.DMA
-    act = jax.ShapeDtypeStruct((width, toks), BF16)
+    act = jax.ShapeDtypeStruct((toks, width), BF16)
     state = pltpu.VMEM((width // 2, 2 * HEAD), F32)
     ring = (2, chips - 1, MSG_SLOTS)
     return pl.pallas_call(
         functools.partial(fused_kernel, devs, scale),
         name='fused',
         in_specs=[pl.BlockSpec(memory_space=pltpu.VMEM)] + [pl.BlockSpec(memory_space=pl.ANY)] * 6,
-        out_specs=[pl.BlockSpec(memory_space=pl.ANY)] * 5,
-        out_shape=[jax.ShapeDtypeStruct((4 * width, width), F32)] + [act] * 4,
+        out_specs=[pl.BlockSpec(memory_space=pl.ANY)] * 3,
+        out_shape=[jax.ShapeDtypeStruct((4 * width, width), F32)] + [act] * 2,
         scratch_shapes=[
             pltpu.VMEM((2, toks, width), BF16),
             pltpu.VMEM((2, 2, QUAD, width), BF16),
@@ -411,9 +477,13 @@
             pltpu.VMEM((8, toks), F32),
             pltpu.VMEM((QUAD, toks), F32),
             pltpu.VMEM((2, QUAD, toks), BF16),
+            pltpu.VMEM((width, toks), BF16),
             pltpu.VMEM((2, QUAD, width), F32),
             pltpu.VMEM((ACC_SLOTS, QUAD // 2, width), F32),
             pltpu.VMEM((2, chips - 1, MSG_SLOTS, piece, width), F32),
+            pltpu.VMEM((toks, width), F32),
+            pltpu.VMEM((toks, width), F32),
+            pltpu.VMEM((2, 128, width), BF16),
             dma((2,)), dma((2, 2)), dma((2,)), dma((2, nquad)), dma((2, nquad)), dma((ACC_SLOTS,)), dma((ACC_SLOTS,)),
             dma(ring), dma(ring), dma(ring), dma(ring), dma((2, MSG_SLOTS)),
             dma((2, chips, MSG_SLOTS)), dma((2, chips, MSG_SLOTS)),
@@ -432,9 +502,7 @@
         scale = 1.0 / (math.sqrt(head_dim) * toks)
         wq, wk, wv = [jnp.transpose(w, (1, 2, 0)).reshape(width, width) for w in (w_q, w_k, w_v)]
         wo = w_o.reshape(width, width)
-        total, ot, dqt, dvt, dkt = fused(devs, scale, flag_loc, x_loc, dy_loc, wq, wk, wv, wo)
-        y_loc = mm(ot, wo, TN).astype(BF16)
-        dx_loc = (mm(dqt, wq, TN) + mm(dkt, wk, TN) + mm(dvt, wv, TN)).astype(BF16)
+        total, y_loc, dx_loc = fused(devs, scale, flag_loc, x_loc, dy_loc, wq, wk, wv, wo)
         dw_o, dw_q, dw_v, dw_k = [total[i * width:(i + 1) * width].reshape(heads, head_dim, width) for i in range(4)]
         dw_q, dw_k, dw_v = [jnp.transpose(dw, (2, 0, 1)) for dw in (dw_q, dw_k, dw_v)]
         return y_loc, dx_loc, dw_q, dw_k, dw_v, dw_o

time: 414 us -> 390 us (0.942)
  matrix products: 27.1 us -> 0 us
    dot_general x4 -> x0, matrix products: 27.1 us -> none  [mm(): return lax.dot_general(lhs, rhs, dims, preferred_element_type=F32)]
where the time goes in v3:
time: 390 us
  Pallas kernels  361 us (93%)
  local copies, waits for them, and re-layouts  28.9 us (7%)
    pallas_call x1, Pallas kernels, fused(): pl.pallas_call(functools.partial(fused_kernel, devs, scale), name='fused'...  361 us
    slice x1, local copies, waits for them, and re-layouts, device_body(): total[i * width:(i + 1) * width].reshape(heads, head_dim, width)  25.6 us

profile of v3, /device:TPU:81, one launch (start us, length us, event | category | flops | bytes accessed | tf_op | source)
XLA Modules:
  0.0 390.4 jit_solution(13236184737820352288)
XLA Ops:
  0.6 360.8 %fused.1 = (f32[6144,1536]{1,0:T(8,128)}, bf16[1024,1536]{1,0:T(8,128)(2,1)}, bf16[1024,1536]{1,0:T(8,128)(2,1)}) custom-call(s32[1,1024]{1,0:T(1,128)} %bitcast.29, bf16[1024,1536]{1,0:T(8,128)(2,1)} %x_ref.1, bf16[1024,1536]{1,0:T(8,128)(2,1)} %dy_ref.1, bf16[1536,1536]{1,0:T(8,128)(2,1)} %bitcast.25, bf16[1536,1536]{1,0:T(8,128)(2,1)} %bitcast.26, ...), custom_call_target="tpu_custom_call" | custom-call | flops 57982058496 | bytes 157286400 | tf_op jit(solution)/shard_map/fused/pallas_call | solution.py:466
  361.4 0.0 copy-start.1
  361.4 0.0 copy-start
  361.5 25.6 %fusion = (f32[1536,1536]{1,0:T(8,128)}, f32[1536,1536]{1,0:T(8,128)}, f32[1536,1536]{1,0:T(8,128)}, f32[1536,1536]{1,0:T(8,128)}) fusion(f32[6144,1536]{1,0:T(8,128)} %get-tuple-element.11), kind=kLoop, calls=%fused_computation | loop fusion | bytes 75497472 | tf_op jit(solution)/shard_map/slice | solution.py:506
  387.0 0.0 copy-done.1
  387.0 1.7 copy.15
  388.7 0.0 copy-done
  388.7 1.7 copy.16
Async XLA Ops:
  361.4 25.6 %copy-start.1 = (bf16[1024,1536]{1,0:T(8,128)(2,1)S(1)}, bf16[1024,1536]{1,0:T(8,128)(2,1)}, u32[]{:S(2)}) copy-start(bf16[1024,1536]{1,0:T(8,128)(2,1)} %get-tuple-element.22) | copy-start | bytes 9437188
  361.4 27.3 %copy-start = (bf16[1024,1536]{1,0:T(8,128)(2,1)S(1)}, bf16[1024,1536]{1,0:T(8,128)(2,1)}, u32[]{:S(2)}) copy-start(bf16[1024,1536]{1,0:T(8,128)(2,1)} %get-tuple-element.23) | copy-start | bytes 9437188

commit v4 on v3

--- a/solution.py
+++ b/solution.py
@@ -16,6 +16,7 @@
 VMEM_CAP = 64 * 1024 * 1024 - 128 * 1024
 ACC_SLOTS = 8
 MSG_SLOTS = 4
+FAST = 4
 
 NN = (((1,), (0,)), ((), ()))
 NT = (((1,), (1,)), ((), ()))
@@ -46,8 +47,8 @@
 
 def fused_kernel(devs, scale, flag_ref, x_ref, dy_ref, wq_ref, wk_ref, wv_ref, wo_ref,
                  out_ref, y_ref, dx_ref,
-                 xy, wbuf, qt, kt, vt, dt, mt, nt, s_in, r_in, s_out, r_out, bound_ref, raw, lhs, ot, part, acc, inbox, y_acc, dx_acc, row_out,
-                 xy_sem, w_sem, row_sem, chain_send, chain_recv, pair_send, pair_recv, rs_send, rs_recv,
+                 xy, wbuf, qt, kt, vt, dt, mt, pre_in, nt, s_got, s_in, r_in, s_out, r_out, bound_ref, raw, lhs, ot, part, acc, inbox, y_acc, dx_acc, row_out,
+                 xy_sem, w_sem, row_sem, pre_send, pre_recv, side_send, chain_send, chain_recv, pair_send, pair_recv, rs_send, rs_recv,
                  ag_send, ag_recv, fin_sem, peer_send, peer_recv):
     width, toks = qt.shape
     nquad = width // QUAD
@@ -63,35 +64,31 @@
     chip = me // 2
     partner = chip * 2 + 1 - core
     targets = (lax.rem(chip + 1, chips) * 2 + core, lax.rem(chip + chips - 1, chips) * 2 + core)
-    up = lax.rem(me + 1, devs)
     down = lax.rem(me + devs - 1, devs)
 
     load_x = pltpu.make_async_copy(x_ref, xy.at[1], xy_sem.at[1])
     load_dy = pltpu.make_async_copy(dy_ref, xy.at[0], xy_sem.at[0])
     load_x.start()
 
-    def w_copies(tick, kv):
-        slot = lax.rem(tick, 2)
-        rows = pl.ds(pl.multiple_of(lax.rem(tick, nquad) * QUAD, QUAD), QUAD)
-        pair = (wk_ref, wv_ref) if kv else (wq_ref, wo_ref)
-        return [pltpu.make_async_copy(ref.at[rows], wbuf.at[slot, i], w_sem.at[slot, i]) for i, ref in enumerate(pair)]
-
-    def start_w(tick):
-        @pl.when(tick < nquad)
-        def _():
-            for copy in w_copies(tick, True):
+    def w_copies(quad, kv):
+        slot = lax.rem(quad, 2)
+        pair, base = ((wk_ref, wv_ref), 0) if kv else ((wq_ref, wo_ref), 2)
+        return [pltpu.make_async_copy(ref.at[pl.ds(pl.multiple_of(quad * QUAD, QUAD), QUAD)], wbuf.at[slot, base + i],
+                                      w_sem.at[slot, base + i]) for i, ref in enumerate(pair)]
+
+    def start_w(quad, kv):
+        @pl.when(quad < nquad)
+        def _():
+            for copy in w_copies(quad, kv):
                 copy.start()
 
-        @pl.when(jnp.logical_and(tick >= nquad, tick < 2 * nquad))
-        def _():
-            for copy in w_copies(tick, False):
-                copy.start()
-
-    start_w(jnp.int32(0))
+    start_w(jnp.int32(0), True)
+    start_w(jnp.int32(0), False)
     load_dy.start()
 
     barrier = pltpu.get_barrier_semaphore()
-    for dev in (up, down, partner) + targets:
+    cross = tuple(lax.rem(chip + hop, chips) * 2 + 1 - core for hop in (1, chips - 1))
+    for dev in (partner,) + targets + cross:
         pl.semaphore_signal(barrier, inc=1, device_id={'sp': dev}, device_id_type=MESH)
 
     lane = lax.broadcasted_iota(jnp.int32, (8, toks), 1)
@@ -117,57 +114,97 @@
     def pack_rows(quad):
         return pl.ds(pl.multiple_of(quad * (QUAD // 2), QUAD // 2), QUAD // 2)
 
-    def project_kv(tick):
-        slot = lax.rem(tick, 2)
-        for copy in w_copies(tick, True):
+    def project_kv(quad):
+        slot = lax.rem(quad, 2)
+        for copy in w_copies(quad, True):
             copy.wait()
-        start_w(tick + 1)
+        start_w(quad + 1, True)
         x_val = xy[1]
         k_val = mm(wbuf[slot, 0], x_val, NT).astype(BF16)
-        kt[quad_rows(tick), :] = k_val
+        kt[quad_rows(quad), :] = k_val
         v_raw = mm(wbuf[slot, 1], x_val, NT)
-        vt[quad_rows(tick), :] = v_raw.astype(BF16)
+        vt[quad_rows(quad), :] = v_raw.astype(BF16)
         tail = pos >= last_bound
-        mt[pack_rows(tick), :] = pack_states(mm(jnp.where(tail, v_raw, 0.0).astype(BF16), k_val, NT))
-
-    def project_qd(tick):
-        slot = lax.rem(tick, 2)
-        quad = tick - nquad
-        for copy in w_copies(tick, False):
+        mt[quad, 0:QUAD // 2, :] = pack_states(mm(jnp.where(tail, v_raw, 0.0).astype(BF16), k_val, NT))
+        mt[quad, QUAD // 2:, :] = jnp.broadcast_to(gate, (8, 2 * HEAD))
+
+        @pl.when(core == 0)
+        def _():
+            pre_copy(quad).start()
+
+    def project_qd(quad):
+        slot = lax.rem(quad, 2)
+        for copy in w_copies(quad, False):
             copy.wait()
-        start_w(tick + 1)
+        start_w(quad + 1, False)
 
         @pl.when(quad == 0)
         def _():
             load_dy.wait()
-        q_val = mm(wbuf[slot, 0], xy[1], NT).astype(BF16)
+        q_val = mm(wbuf[slot, 2], xy[1], NT).astype(BF16)
         qt[quad_rows(quad), :] = q_val
-        d_raw = mm(wbuf[slot, 1], xy[0], NT)
+        d_raw = mm(wbuf[slot, 3], xy[0], NT)
         dt[quad_rows(quad), :] = d_raw.astype(BF16)
         nt[pack_rows(quad), :] = pack_states(mm(jnp.where(bound < 0.0, d_raw, 0.0).astype(BF16), q_val, NT))
 
-    def chain_copy(way, quad):
+    def pre_copy(quad):
+        return pltpu.make_async_remote_copy(src_ref=mt.at[quad], dst_ref=pre_in.at[quad], send_sem=pre_send.at[quad],
+                                            recv_sem=pre_recv.at[quad], device_id={'sp': partner}, device_id_type=MESH)
+
+    def state_copy(quad, same_core):
         rows = pack_rows(quad)
-        src, dst, dev = ((s_out, s_in, up), (r_out, r_in, down))[way]
-        return pltpu.make_async_remote_copy(src_ref=src.at[rows], dst_ref=dst.at[rows], send_sem=chain_send.at[way, quad],
-                                            recv_sem=chain_recv.at[way, quad], device_id={'sp': dev}, device_id_type=MESH)
-
-    def chain_step(way, quad, first, final):
+        base = lax.rem(chip + 1, chips) * 2
+        dev, sem = (base + 1, chain_send.at[0, quad]) if same_core else (base, side_send.at[quad])
+        return pltpu.make_async_remote_copy(src_ref=s_out.at[rows], dst_ref=s_got.at[rows], send_sem=sem,
+                                            recv_sem=chain_recv.at[0, quad], device_id={'sp': dev}, device_id_type=MESH)
+
+    def state_step(quad):
         rows = pack_rows(quad)
-        own, got, nxt = ((mt, s_in, s_out), (nt, r_in, r_out))[way]
-
-        @pl.when(first)
-        def _():
-            got[rows, :] = jnp.zeros((QUAD // 2, 2 * HEAD), F32)
-
-        @pl.when(jnp.logical_not(first))
-        def _():
-            chain_copy(way, quad).wait_recv()
-
-        @pl.when(jnp.logical_not(final))
-        def _():
-            nxt[rows, :] = gate * got[rows, :] + own[rows, :]
-            chain_copy(way, quad).start()
+
+        @pl.when(chip == 0)
+        def _():
+            s_got[rows, :] = jnp.zeros((QUAD // 2, 2 * HEAD), F32)
+
+        @pl.when(chip > 0)
+        def _():
+            state_copy(quad, True).wait_recv()
+
+        @pl.when(core == 0)
+        def _():
+            s_in[rows, :] = s_got[rows, :]
+
+        @pl.when(core == 1)
+        def _():
+            pre_copy(quad).wait_recv()
+            mine = pre_in[quad, QUAD // 2:QUAD // 2 + 1, :] * s_got[rows, :] + pre_in[quad, 0:QUAD // 2, :]
+            s_in[rows, :] = mine
+
+            @pl.when(chip < chips - 1)
+            def _():
+                s_out[rows, :] = gate * mine + mt[quad, 0:QUAD // 2, :]
+                state_copy(quad, True).start()
+                state_copy(quad, False).start()
+
+    def chain_copy(quad):
+        rows = pack_rows(quad)
+        return pltpu.make_async_remote_copy(src_ref=r_out.at[rows], dst_ref=r_in.at[rows], send_sem=chain_send.at[1, quad],
+                                            recv_sem=chain_recv.at[1, quad], device_id={'sp': down}, device_id_type=MESH)
+
+    def chain_step(quad):
+        rows = pack_rows(quad)
+
+        @pl.when(me == devs - 1)
+        def _():
+            r_in[rows, :] = jnp.zeros((QUAD // 2, 2 * HEAD), F32)
+
+        @pl.when(me < devs - 1)
+        def _():
+            chain_copy(quad).wait_recv()
+
+        @pl.when(me > 0)
+        def _():
+            r_out[rows, :] = gate * r_in[rows, :] + nt[rows, :]
+            chain_copy(quad).start()
 
     def remote(src, dst, s_sem, r_sem, dev):
         return pltpu.make_async_remote_copy(src_ref=src, dst_ref=dst, send_sem=s_sem, recv_sem=r_sem,
@@ -325,12 +362,14 @@
             if kind == 0:
                 ot[quad_rows(quad), cols] = lhs[slot, :, cols]
 
+    def stage_unit(idx):
+        for kind in range(4):
+            @pl.when(idx // nquad == kind)
+            def _():
+                unit(idx, kind)
+
     def stage_partial(idx):
         slot = lax.rem(idx, 2)
-        for kind in range(4):
-            @pl.when(idx // nquad == kind)
-            def _():
-                unit(idx, kind)
         rhs_id = jnp.minimum(idx // nquad, 1)
         tile_n = 512 if width % 512 == 0 else width
 
@@ -411,45 +450,58 @@
     for step in reversed(range(1, chips)):
         order.append((1 + step, functools.partial(stage_reduce, step=step)))
     order.append((1, stage_pair))
-    order.append((0, stage_partial))
-    lead = max(devs - 1, nquad)
+    lead = chips
+
+    def when_in(idx, limit, body):
+        @pl.when(jnp.logical_and(idx >= 0, idx < limit))
+        def _():
+            body(idx)
 
     def tick_step(tick, carry):
-        @pl.when(tick < nquad)
-        def _():
-            project_kv(tick)
-
-        @pl.when(jnp.logical_and(tick >= nquad, tick < 2 * nquad))
-        def _():
-            project_qd(tick)
-        s_quad = tick - me
-        r_quad = tick - nquad - (devs - 1 - me)
-
-        @pl.when(jnp.logical_and(s_quad >= 0, s_quad < nquad))
-        def _():
-            chain_step(0, s_quad, me == 0, me == devs - 1)
-
-        @pl.when(jnp.logical_and(r_quad >= 0, r_quad < nquad))
-        def _():
-            chain_step(1, r_quad, me == devs - 1, me == 0)
-        for delay, stage in order:
-            idx = tick - lead - delay
-
-            @pl.when(jnp.logical_and(idx >= 0, idx < count))
-            def _():
-                stage(idx)
+        when_in(tick, nquad, project_kv)
+        when_in(tick - lead, nquad, project_qd)
+        when_in(tick - 1 - chip, nquad, state_step)
+        when_in(tick - lead - (devs - 1 - me), nquad, chain_step)
+        rnd = tick - lead
+
+        def poll(turn, carry):
+            for delay, stage in order:
+                slow = rnd - delay
+                quick = rnd - (delay + 1) // 2
+                on_turn = turn == (0 if delay % 2 else 1)
+                is_quick = jnp.logical_and(on_turn, jnp.logical_and(quick >= 0, quick < FAST))
+                is_slow = jnp.logical_and(turn == 0, jnp.logical_and(slow >= FAST, slow < count))
+
+                @pl.when(jnp.logical_or(is_quick, is_slow))
+                def _():
+                    stage(jnp.where(is_quick, quick, slow))
+
+            @pl.when(turn == 0)
+            def _():
+                when_in(rnd, count, stage_unit)
+
+            @pl.when(turn == 1)
+            def _():
+                when_in(rnd, count, stage_partial)
+            return carry
+        lax.fori_loop(0, 2, poll, 0)
         return carry
 
     lax.fori_loop(0, lead + count + 2 * chips, tick_step, 0)
 
     def chain_end(quad, carry):
-        @pl.when(me < devs - 1)
-        def _():
-            chain_copy(0, quad).wait_send()
+        @pl.when(core == 0)
+        def _():
+            pre_copy(quad).wait_send()
+
+        @pl.when(jnp.logical_and(core == 1, chip < chips - 1))
+        def _():
+            state_copy(quad, True).wait_send()
+            state_copy(quad, False).wait_send()
 
         @pl.when(me > 0)
         def _():
-            chain_copy(1, quad).wait_send()
+            chain_copy(quad).wait_send()
         return carry
     lax.fori_loop(0, nquad, chain_end, 0)
 
@@ -471,8 +523,10 @@
         out_shape=[jax.ShapeDtypeStruct((4 * width, width), F32)] + [act] * 2,
         scratch_shapes=[
             pltpu.VMEM((2, toks, width), BF16),
-            pltpu.VMEM((2, 2, QUAD, width), BF16),
+            pltpu.VMEM((2, 4, QUAD, width), BF16),
             *[pltpu.VMEM((width, toks), BF16)] * 4,
+            pltpu.VMEM((nquad, QUAD // 2 + 8, 2 * HEAD), F32),
+            pltpu.VMEM((nquad, QUAD // 2 + 8, 2 * HEAD), F32),
             *[state] * 6,
             pltpu.VMEM((8, toks), F32),
             pltpu.VMEM((QUAD, toks), F32),
@@ -484,7 +538,7 @@
             pltpu.VMEM((toks, width), F32),
             pltpu.VMEM((toks, width), F32),
             pltpu.VMEM((2, 128, width), BF16),
-            dma((2,)), dma((2, 2)), dma((2,)), dma((2, nquad)), dma((2, nquad)), dma((ACC_SLOTS,)), dma((ACC_SLOTS,)),
+            dma((2,)), dma((2, 4)), dma((2,)), dma((nquad,)), dma((nquad,)), dma((nquad,)), dma((2, nquad)), dma((2, nquad)), dma((ACC_SLOTS,)), dma((ACC_SLOTS,)),
             dma(ring), dma(ring), dma(ring), dma(ring), dma((2, MSG_SLOTS)),
             dma((2, chips, MSG_SLOTS)), dma((2, chips, MSG_SLOTS)),
         ],

time: 390 us -> 392 us (level)
  no operation moved by 1% of the time
where the time goes in v4:
time: 392 us
  Pallas kernels  362 us (92%)
  local copies, waits for them, and re-layouts  28.9 us (7%)
    pallas_call x1, Pallas kernels, fused(): pl.pallas_call(functools.partial(fused_kernel, devs, scale), name='fused'...  362 us
    slice x1, local copies, waits for them, and re-layouts, device_body(): total[i * width:(i + 1) * width].reshape(heads, head_dim, width)  25.6 us

profile of v4, /device:TPU:81, one launch (start us, length us, event | category | flops | bytes accessed | tf_op | source)
XLA Modules:
  0.0 391.6 jit_solution(3841342318112252280)
XLA Ops:
  0.6 362.1 %fused.1 = (f32[6144,1536]{1,0:T(8,128)}, bf16[1024,1536]{1,0:T(8,128)(2,1)}, bf16[1024,1536]{1,0:T(8,128)(2,1)}) custom-call(s32[1,1024]{1,0:T(1,128)} %bitcast.29, bf16[1024,1536]{1,0:T(8,128)(2,1)} %x_ref.1, bf16[1024,1536]{1,0:T(8,128)(2,1)} %dy_ref.1, bf16[1536,1536]{1,0:T(8,128)(2,1)} %bitcast.25, bf16[1536,1536]{1,0:T(8,128)(2,1)} %bitcast.26, ...), custom_call_target="tpu_custom_call" | custom-call | flops 57982058496 | bytes 157286400 | tf_op jit(solution)/shard_map/fused/pallas_call | solution.py:518
  362.7 0.0 copy-start.1
  362.7 0.0 copy-start
  362.7 25.6 %fusion = (f32[1536,1536]{1,0:T(8,128)}, f32[1536,1536]{1,0:T(8,128)}, f32[1536,1536]{1,0:T(8,128)}, f32[1536,1536]{1,0:T(8,128)}) fusion(f32[6144,1536]{1,0:T(8,128)} %get-tuple-element.11), kind=kLoop, calls=%fused_computation | loop fusion | bytes 75497472 | tf_op jit(solution)/shard_map/slice | solution.py:560
  388.3 0.0 copy-done.1
  388.3 1.7 copy.15
  390.0 0.0 copy-done
  390.0 1.7 copy.16
Async XLA Ops:
  362.7 25.6 %copy-start.1 = (bf16[1024,1536]{1,0:T(8,128)(2,1)S(1)}, bf16[1024,1536]{1,0:T(8,128)(2,1)}, u32[]{:S(2)}) copy-start(bf16[1024,1536]{1,0:T(8,128)(2,1)} %get-tuple-element.22) | copy-start | bytes 9437188
  362.7 27.3 %copy-start = (bf16[1024,1536]{1,0:T(8,128)(2,1)S(1)}, bf16[1024,1536]{1,0:T(8,128)(2,1)}, u32[]{:S(2)}) copy-start(bf16[1024,1536]{1,0:T(8,128)(2,1)} %get-tuple-element.23) | copy-start | bytes 9437188

commit v5 on v4

--- a/solution.py
+++ b/solution.py
@@ -17,6 +17,7 @@
 ACC_SLOTS = 8
 MSG_SLOTS = 4
 FAST = 4
+LATE = 3
 
 NN = (((1,), (0,)), ((), ()))
 NT = (((1,), (1,)), ((), ()))
@@ -70,20 +71,22 @@
     load_dy = pltpu.make_async_copy(dy_ref, xy.at[0], xy_sem.at[0])
     load_x.start()
 
-    def w_copies(quad, kv):
+    weights = (wk_ref, wv_ref, wq_ref, wo_ref)
+
+    def w_copy(quad, which):
         slot = lax.rem(quad, 2)
-        pair, base = ((wk_ref, wv_ref), 0) if kv else ((wq_ref, wo_ref), 2)
-        return [pltpu.make_async_copy(ref.at[pl.ds(pl.multiple_of(quad * QUAD, QUAD), QUAD)], wbuf.at[slot, base + i],
-                                      w_sem.at[slot, base + i]) for i, ref in enumerate(pair)]
-
-    def start_w(quad, kv):
+        return pltpu.make_async_copy(weights[which].at[pl.ds(pl.multiple_of(quad * QUAD, QUAD), QUAD)], wbuf.at[slot, which],
+                                     w_sem.at[slot, which])
+
+    def start_w(quad, which):
         @pl.when(quad < nquad)
         def _():
-            for copy in w_copies(quad, kv):
-                copy.start()
-
-    start_w(jnp.int32(0), True)
-    start_w(jnp.int32(0), False)
+            w_copy(quad, which).start()
+
+    start_w(jnp.int32(0), 0)
+    start_w(jnp.int32(0), 1)
+    start_w(jnp.int32(0), 2)
+    start_w(jnp.int32(0), 3)
     load_dy.start()
 
     barrier = pltpu.get_barrier_semaphore()
@@ -116,9 +119,9 @@
 
     def project_kv(quad):
         slot = lax.rem(quad, 2)
-        for copy in w_copies(quad, True):
-            copy.wait()
-        start_w(quad + 1, True)
+        for which in range(2):
+            w_copy(quad, which).wait()
+            start_w(quad + 1, which)
         x_val = xy[1]
         k_val = mm(wbuf[slot, 0], x_val, NT).astype(BF16)
         kt[quad_rows(quad), :] = k_val
@@ -132,20 +135,17 @@
         def _():
             pre_copy(quad).start()
 
-    def project_qd(quad):
-        slot = lax.rem(quad, 2)
-        for copy in w_copies(quad, False):
-            copy.wait()
-        start_w(quad + 1, False)
-
-        @pl.when(quad == 0)
-        def _():
-            load_dy.wait()
-        q_val = mm(wbuf[slot, 2], xy[1], NT).astype(BF16)
-        qt[quad_rows(quad), :] = q_val
-        d_raw = mm(wbuf[slot, 3], xy[0], NT)
+    def project_q(quad):
+        w_copy(quad, 2).wait()
+        start_w(quad + 1, 2)
+        qt[quad_rows(quad), :] = mm(wbuf[lax.rem(quad, 2), 2], xy[1], NT).astype(BF16)
+
+    def project_d(quad):
+        w_copy(quad, 3).wait()
+        start_w(quad + 1, 3)
+        d_raw = mm(wbuf[lax.rem(quad, 2), 3], xy[0], NT)
         dt[quad_rows(quad), :] = d_raw.astype(BF16)
-        nt[pack_rows(quad), :] = pack_states(mm(jnp.where(bound < 0.0, d_raw, 0.0).astype(BF16), q_val, NT))
+        nt[pack_rows(quad), :] = pack_states(mm(jnp.where(bound < 0.0, d_raw, 0.0).astype(BF16), qt[quad_rows(quad), :], NT))
 
     def pre_copy(quad):
         return pltpu.make_async_remote_copy(src_ref=mt.at[quad], dst_ref=pre_in.at[quad], send_sem=pre_send.at[quad],
@@ -257,26 +257,38 @@
     def post_copies(idx):
         slot = lax.rem(idx, 2)
         rows = quad_rows(lax.rem(idx, nquad))
-        y_copy = pltpu.make_async_copy(wo_ref.at[rows], wbuf.at[slot, 1], w_sem.at[slot, 1])
-        return [pltpu.make_async_copy(ref.at[rows], wbuf.at[slot, 0], w_sem.at[slot, 0]) for ref in (wq_ref, wv_ref, wk_ref)], y_copy
+        return [pltpu.make_async_copy(ref.at[rows], wbuf.at[slot, 0], w_sem.at[slot, 0]) for ref in (wq_ref, wv_ref, wk_ref)]
 
     def start_post(idx):
-        dx_copies, y_copy = post_copies(idx)
         for kind in range(1, 4):
             @pl.when(idx // nquad == kind)
             def _():
-                dx_copies[kind - 1].start()
-
-        @pl.when(idx // nquad == 2)
-        def _():
-            y_copy.start()
-
-    def accumulate(total, rows_t, weight, fresh):
-        tile_t = 256
+                post_copies(idx)[kind - 1].start()
+
+    def y_copies(idx):
+        slot = lax.rem(idx, 2)
+        return [pltpu.make_async_copy(wo_ref.at[quad_rows(2 * idx + i)], wbuf.at[slot, 2 + i], w_sem.at[slot, 2 + i]) for i in range(2)]
+
+    def stage_y(idx):
+        for copy in y_copies(idx):
+            copy.wait()
+
+        @pl.when(idx + 1 < nquad // 2)
+        def _():
+            for copy in y_copies(idx + 1):
+                copy.start()
+        accumulate(y_acc, [(ot.at[quad_rows(2 * idx + i)], wbuf.at[lax.rem(idx, 2), 2 + i]) for i in range(2)], idx == 0)
+
+        @pl.when(idx == nquad // 2 - 1)
+        def _():
+            write_rows(y_acc, y_ref)
+
+    def accumulate(total, terms, fresh):
+        tile_t = 128
 
         def tile(step, carry):
             toks_at = pl.ds(pl.multiple_of(step * tile_t, tile_t), tile_t)
-            add = mm(rows_t[:, toks_at], weight[...], TN)
+            add = mm(terms[0][0][:, toks_at], terms[0][1][...], TN) + mm(terms[1][0][:, toks_at], terms[1][1][...], TN)
 
             @pl.when(fresh)
             def _():
@@ -300,27 +312,20 @@
             pltpu.make_async_copy(row_out.at[i], dst.at[i * tile_t:(i + 1) * tile_t], row_sem.at[i]).wait()
 
     def stage_post(idx):
-        slot = lax.rem(idx, 2)
-        kind = idx // nquad
-        dx_copies, y_copy = post_copies(idx)
-        dx_copies[0].wait()
+        post_copies(idx)[0].wait()
+
+        @pl.when(lax.rem(idx, 2) == 1)
+        def _():
+            accumulate(dx_acc, [(lhs.at[slot], wbuf.at[slot, 0]) for slot in range(2)], idx == nquad + 1)
 
         @pl.when(idx + 1 < count)
         def _():
             start_post(idx + 1)
-        accumulate(dx_acc, lhs.at[slot], wbuf.at[slot, 0], idx == nquad)
-
-        @pl.when(kind == 2)
-        def _():
-            y_copy.wait()
-            accumulate(y_acc, ot.at[quad_rows(lax.rem(idx, nquad))], wbuf.at[slot, 1], idx == 2 * nquad)
-
-        @pl.when(idx == 3 * nquad)
-        def _():
-            write_rows(y_acc, y_ref)
 
         @pl.when(idx == count - 1)
         def _():
+            for copy in y_copies(jnp.int32(0)):
+                copy.start()
             write_rows(dx_acc, dx_ref)
 
     def unit(idx, kind):
@@ -370,8 +375,12 @@
 
     def stage_partial(idx):
         slot = lax.rem(idx, 2)
+
+        @pl.when(idx == 0)
+        def _():
+            load_dy.wait()
         rhs_id = jnp.minimum(idx // nquad, 1)
-        tile_n = 512 if width % 512 == 0 else width
+        tile_n = width // 2
 
         def tile(step, carry):
             cols = pl.ds(pl.multiple_of(step * tile_n, tile_n), tile_n)
@@ -459,9 +468,10 @@
 
     def tick_step(tick, carry):
         when_in(tick, nquad, project_kv)
-        when_in(tick - lead, nquad, project_qd)
+        when_in(tick - lead, nquad, project_q)
+        when_in(tick - lead - LATE, nquad, project_d)
         when_in(tick - 1 - chip, nquad, state_step)
-        when_in(tick - lead - (devs - 1 - me), nquad, chain_step)
+        when_in(tick - lead - LATE - (devs - 1 - me), nquad, chain_step)
         rnd = tick - lead
 
         def poll(turn, carry):
@@ -483,6 +493,7 @@
             @pl.when(turn == 1)
             def _():
                 when_in(rnd, count, stage_partial)
+                when_in(rnd - count, nquad // 2, stage_y)
             return carry
         lax.fori_loop(0, 2, poll, 0)
         return carry

time: 392 us -> 395 us (level)
  no operation moved by 1% of the time
where the time goes in v5:
time: 395 us
  Pallas kernels  365 us (92%)
  local copies, waits for them, and re-layouts  28.9 us (7%)
    pallas_call x1, Pallas kernels, fused(): pl.pallas_call(functools.partial(fused_kernel, devs, scale), name='fused'...  365 us
    slice x1, local copies, waits for them, and re-layouts, device_body(): total[i * width:(i + 1) * width].reshape(heads, head_dim, width)  25.6 us

profile of v5, /device:TPU:81, one launch (start us, length us, event | category | flops | bytes accessed | tf_op | source)
XLA Modules:
  0.0 394.6 jit_solution(13232543538950476744)
XLA Ops:
  0.6 365.0 %fused.1 = (f32[6144,1536]{1,0:T(8,128)}, bf16[1024,1536]{1,0:T(8,128)(2,1)}, bf16[1024,1536]{1,0:T(8,128)(2,1)}) custom-call(s32[1,1024]{1,0:T(1,128)} %bitcast.29, bf16[1024,1536]{1,0:T(8,128)(2,1)} %x_ref.1, bf16[1024,1536]{1,0:T(8,128)(2,1)} %dy_ref.1, bf16[1536,1536]{1,0:T(8,128)(2,1)} %bitcast.25, bf16[1536,1536]{1,0:T(8,128)(2,1)} %bitcast.26, ...), custom_call_target="tpu_custom_call" | custom-call | flops 57982058496 | bytes 157286400 | tf_op jit(solution)/shard_map/fused/pallas_call | solution.py:529
  365.7 0.0 copy-start.1
  365.7 0.0 copy-start
  365.7 25.6 %fusion = (f32[1536,1536]{1,0:T(8,128)}, f32[1536,1536]{1,0:T(8,128)}, f32[1536,1536]{1,0:T(8,128)}, f32[1536,1536]{1,0:T(8,128)}) fusion(f32[6144,1536]{1,0:T(8,128)} %get-tuple-element.11), kind=kLoop, calls=%fused_computation | loop fusion | bytes 75497472 | tf_op jit(solution)/shard_map/slice | solution.py:571
  391.3 0.0 copy-done.1
  391.3 1.7 copy.15
  392.9 0.0 copy-done
  392.9 1.7 copy.16
Async XLA Ops:
  365.7 25.6 %copy-start.1 = (bf16[1024,1536]{1,0:T(8,128)(2,1)S(1)}, bf16[1024,1536]{1,0:T(8,128)(2,1)}, u32[]{:S(2)}) copy-start(bf16[1024,1536]{1,0:T(8,128)(2,1)} %get-tuple-element.22) | copy-start | bytes 9437188
  365.7 27.3 %copy-start = (bf16[1024,1536]{1,0:T(8,128)(2,1)S(1)}, bf16[1024,1536]{1,0:T(8,128)(2,1)}, u32[]{:S(2)}) copy-start(bf16[1024,1536]{1,0:T(8,128)(2,1)} %get-tuple-element.23) | copy-start | bytes 9437188

commit v6 on v5

--- a/solution.py
+++ b/solution.py
@@ -322,10 +322,18 @@
         def _():
             start_post(idx + 1)
 
-        @pl.when(idx == count - 1)
+        @pl.when(idx == 2 * nquad - 1)
         def _():
             for copy in y_copies(jnp.int32(0)):
                 copy.start()
+        turn_y = idx - 2 * nquad
+
+        @pl.when(jnp.logical_and(lax.rem(idx, 2) == 0, jnp.logical_and(turn_y >= 0, turn_y < nquad)))
+        def _():
+            stage_y(turn_y // 2)
+
+        @pl.when(idx == count - 1)
+        def _():
             write_rows(dx_acc, dx_ref)
 
     def unit(idx, kind):
@@ -493,7 +501,6 @@
             @pl.when(turn == 1)
             def _():
                 when_in(rnd, count, stage_partial)
-                when_in(rnd - count, nquad // 2, stage_y)
             return carry
         lax.fori_loop(0, 2, poll, 0)
         return carry

time: 395 us -> 392 us (level)
  no operation moved by 1% of the time
where the time goes in v6:
time: 392 us
  Pallas kernels  362 us (92%)
  local copies, waits for them, and re-layouts  28.9 us (7%)
    pallas_call x1, Pallas kernels, fused(): pl.pallas_call(functools.partial(fused_kernel, devs, scale), name='fused'...  362 us
    slice x1, local copies, waits for them, and re-layouts, device_body(): total[i * width:(i + 1) * width].reshape(heads, head_dim, width)  25.6 us

profile of v6, /device:TPU:81, one launch (start us, length us, event | category | flops | bytes accessed | tf_op | source)
XLA Modules:
  0.0 392.0 jit_solution(12812999216398315598)
XLA Ops:
  0.6 362.4 %fused.1 = (f32[6144,1536]{1,0:T(8,128)}, bf16[1024,1536]{1,0:T(8,128)(2,1)}, bf16[1024,1536]{1,0:T(8,128)(2,1)}) custom-call(s32[1,1024]{1,0:T(1,128)} %bitcast.29, bf16[1024,1536]{1,0:T(8,128)(2,1)} %x_ref.1, bf16[1024,1536]{1,0:T(8,128)(2,1)} %dy_ref.1, bf16[1536,1536]{1,0:T(8,128)(2,1)} %bitcast.25, bf16[1536,1536]{1,0:T(8,128)(2,1)} %bitcast.26, ...), custom_call_target="tpu_custom_call" | custom-call | flops 57982058496 | bytes 157286400 | tf_op jit(solution)/shard_map/fused/pallas_call | solution.py:536
  363.0 0.0 copy-start.1
  363.1 0.0 copy-start
  363.1 25.6 %fusion = (f32[1536,1536]{1,0:T(8,128)}, f32[1536,1536]{1,0:T(8,128)}, f32[1536,1536]{1,0:T(8,128)}, f32[1536,1536]{1,0:T(8,128)}) fusion(f32[6144,1536]{1,0:T(8,128)} %get-tuple-element.11), kind=kLoop, calls=%fused_computation | loop fusion | bytes 75497472 | tf_op jit(solution)/shard_map/slice | solution.py:578
  388.6 0.0 copy-done.1
  388.6 1.7 copy.15
  390.3 0.0 copy-done
  390.3 1.7 copy.16
Async XLA Ops:
  363.0 25.6 %copy-start.1 = (bf16[1024,1536]{1,0:T(8,128)(2,1)S(1)}, bf16[1024,1536]{1,0:T(8,128)(2,1)}, u32[]{:S(2)}) copy-start(bf16[1024,1536]{1,0:T(8,128)(2,1)} %get-tuple-element.22) | copy-start | bytes 9437188
  363.1 27.3 %copy-start = (bf16[1024,1536]{1,0:T(8,128)(2,1)S(1)}, bf16[1024,1536]{1,0:T(8,128)(2,1)}, u32[]{:S(2)}) copy-start(bf16[1024,1536]{1,0:T(8,128)(2,1)} %get-tuple-element.23) | copy-start | bytes 9437188
